TPU v7x, 512 devices: a whole 4x8x8 slice. The times are simulated.
512 devices in a mesh: grid: 64 (over y, z_hi, core), vec: 8 (over x, z_lo).
Axes of the slice: x: 4, y: 8, z: 8 (z_hi: 4, z_lo: 2; z = z_hi * 2 + z_lo), core: 2. Of those that a mesh axis runs over, the one named last changes fastest.
Arguments:
- tgt_coords: float32 [3, 8192], P(None, 'grid'), may hold values from 0 to 1
- src_coords: float32 [3, 8192], P(None, 'grid'), may hold values from 0 to 1
- src_values: float32 [2048, 8192], P('vec', 'grid'), may hold values from -0.26516503 to 0.26516503
- grad_vectors: float32 [3, 2048, 8192], P(None, 'vec', 'grid'), may hold values from -0.75 to 0.75
Outputs:
- interaction: float32 [2048, 2048], P('grid', 'vec')
All inputs are finite; a program needn't handle non-finite values.
Results may differ from a plain program's by a relative error of at most 0.00023.
Values sent between devices are 32-bit elements; how exact they have to be, the bound alone decides.
No kernel may reach another device: no remote copies, remote signals or barrier semaphores. Data moves between devices by JAX's collectives and lax.ppermute only.
A program may use at most 64 MiB of HBM per device.

v0:
```python
import math

import jax
import jax.numpy as jnp
from jax import lax
from jax.sharding import PartitionSpec as P

stiff = 1.0
soft = 0.05


def in_one_piece(arrays, axis, dim, along):
    ends, at = ([], 0)
    for a in arrays[:-1]:
        at += a.shape[along]
        ends.append(at)
    both = jnp.concatenate(arrays, axis=along)
    return tuple(jnp.split(lax.all_gather(both, axis, axis=dim, tiled=True), ends, axis=along))


def cut_along(array, dim, peers):
    shape = array.shape
    blocks = array.reshape(*shape[:dim], peers, shape[dim] // peers, *shape[dim + 1 :])
    return jnp.moveaxis(blocks, dim, 0)


def sum_at_owner(array, axis, dim):
    blocks = cut_along(array, dim, lax.axis_size(axis))
    arrived = lax.all_to_all(blocks, axis, split_axis=0, concat_axis=0, tiled=True)
    return arrived.sum(axis=0)


def pair_kernel(targets, sources):
    diff = targets[:, :, None] - sources[:, None, :]
    dist2 = jnp.sum(diff * diff, axis=0)
    scale = 0.5 / ((1.0 + stiff * jnp.sqrt(dist2)) ** 2 * jnp.sqrt(dist2 + soft * soft))
    return diff * scale[None, :, :]


def body(tgt_coords, src_coords, src_values, grad_vectors):
    width = src_values.shape[0]
    tgt_rows = tgt_coords.shape[1]
    gathered = lax.all_gather(grad_vectors, "vec", axis=1, tiled=True)
    start_sum = jnp.zeros((3, tgt_rows, width), jnp.float32)
    total = start_sum
    coords, values = in_one_piece((src_coords, src_values), "grid", 1, 0)
    count = coords.shape[1]
    block_len = math.gcd(count, 512)
    nblocks = count // block_len
    coord_blocks = coords.reshape(3, nblocks, block_len).transpose(1, 0, 2)
    value_blocks = values.reshape(width, nblocks, block_len).transpose(1, 0, 2)

    def inner(carry, items):
        cblock, vblock = items
        kern = pair_kernel(tgt_coords, cblock)
        carry = carry + jnp.einsum("cts,qs->ctq", kern, vblock, precision=lax.Precision.HIGHEST)
        return (carry, None)

    total, _ = lax.scan(inner, total, (coord_blocks, value_blocks))
    partial_value = jnp.einsum("cpt,ctq->pq", gathered, total, precision=lax.Precision.HIGHEST)
    return sum_at_owner(partial_value, "grid", 0)


def solution(mesh):
    return jax.shard_map(
        body,
        mesh=mesh,
        in_specs=(P(None, "grid"), P(None, "grid"), P("vec", "grid"), P(None, "vec", "grid")),
        out_specs=P("grid", "vec"),
        check_vma=False,
    )
```

profile of v0, /device:TPU:24, one launch (start us, length us, event | category | flops | bytes accessed | tf_op | source)
XLA Modules:
  0.0 294.5 jit_solution(4307227119990213914)
XLA Ops:
  6.5 1.0 copy.7
  7.5 0.8 copy.6
  8.3 0.8 pad_maximum_fusion
  9.2 0.7 all-gather.5.cloned.1.call-update
  9.9 126.4 %all-gather.3.cloned.1.call-done = f32[259,8192]{0,1:T(8,128)} async-done(((f32[259,128]{0,1:T(8,128)}), f32[259,8192]{0,1:T(8,128)}) %all-gather.3.cloned.1.call-update) | async-done | bytes 8486928 | tf_op jit(solution)/shard_map/all_gather | solution.py:18
  136.3 4.4 %split.8 = f32[3,8192]{0,1:T(8,128)} slice(f32[259,8192]{0,1:T(8,128)} %all-gather.3.cloned.1.call-done), slice={[0:3], [0:8192]} | slice | bytes 196608 | tf_op jit(solution)/shard_map/split | solution.py:18
  140.7 2.8 copy.8
  143.6 10.0 %split.9 = f32[256,8192]{0,1:T(8,128)} slice(f32[259,8192]{0,1:T(8,128)} %all-gather.3.cloned.1.call-done), slice={[3:259], [0:8192]} | slice | bytes 16777216 | tf_op jit(solution)/shard_map/split | solution.py:18
  153.6 38.8 %while.11 = (s32[]{:T(128)}, f32[3,128,256]{2,1,0:T(8,128)S(1)}, f32[3,128]{1,0:T(4,128)S(1)}, f32[16,3,512]{2,1,0:T(4,128)S(1)}, f32[16,256,512]{1,2,0:T(8,128)}, /*index=5*/s32[]{:T(128)}, s32[]{:T(128)}) while((s32[]{:T(128)}, f32[3,128,256]{2,1,0:T(8,128)S(1)}, f32[3,128]{1,0:T(4,128)S(1)}, f32[16,3,512]{2,1,0:T(4,128)S(1)}, ...), condition=%wide.region_2.3_spmd.clone, body=%wide.region_0.2_spmd.clone.sunk | while | flops 605421568 | bytes 2387047 | solution.py:59
  153.6 0.1 fusion.12
  153.7 0.2 multiply_divide_fusion.2
  153.9 2.0 convolution_add_fusion.2
  156.0 0.1 fusion.12
  156.2 0.2 multiply_divide_fusion.2
  156.3 2.1 convolution_add_fusion.2
  158.6 0.2 multiply_divide_fusion.2
  158.8 2.1 convolution_add_fusion.2
  161.0 0.2 multiply_divide_fusion.2
  161.2 2.0 convolution_add_fusion.2
  163.5 0.2 multiply_divide_fusion.2
  163.6 2.0 convolution_add_fusion.2
  165.9 0.2 multiply_divide_fusion.2
  166.1 2.0 convolution_add_fusion.2
  168.3 0.2 multiply_divide_fusion.2
  168.5 2.0 convolution_add_fusion.2
  170.7 0.2 multiply_divide_fusion.2
  170.9 2.0 convolution_add_fusion.2
  173.2 0.2 multiply_divide_fusion.2
  173.3 2.1 convolution_add_fusion.2
  175.6 0.2 multiply_divide_fusion.2
  175.8 2.1 convolution_add_fusion.2
  178.0 0.2 multiply_divide_fusion.2
  178.2 2.0 convolution_add_fusion.2
  180.4 0.2 multiply_divide_fusion.2
  180.6 2.0 convolution_add_fusion.2
  182.9 0.2 multiply_divide_fusion.2
  183.1 2.0 convolution_add_fusion.2
  185.3 0.2 multiply_divide_fusion.2
  185.5 2.0 convolution_add_fusion.2
  187.7 0.2 multiply_divide_fusion.2
  187.9 2.1 convolution_add_fusion.2
  190.2 0.2 multiply_divide_fusion.2
  190.4 2.1 convolution_add_fusion.2
  192.4 18.9 %all-gather.5.cloned.1.call-done = f32[3,2048,128]{2,1,0:T(8,128)} async-done(((f32[3,256,128]{2,1,0:T(8,128)}), f32[3,2048,128]{2,1,0:T(8,128)}) %all-gather.5.cloned.1.call-update) | async-done | bytes 3145744 | tf_op jit(solution)/shard_map/all_gather | solution.py:43
  211.3 7.1 %convolution_bitcast_fusion = f32[2048,256]{0,1:T(8,128)S(1)} fusion(f32[3,128,256]{2,1,0:T(8,128)S(1)} %get-tuple-element.32, f32[3,2048,128]{2,1,0:T(8,128)} %all-gather.5.cloned.1.call-done), kind=kOutput, calls=%fused_computation.12 | convolution fusion | flops 2415919104 | bytes 5636096 | tf_op jit(solution)/shard_map/cpt,ctq->pq/dot_general | solution.py:60
  218.5 1.9 copy.11
  220.3 66.6 %all_to_all.5 = f32[64,32,256]{2,1,0:T(8,128)S(1)} all-to-all(f32[64,32,256]{2,1,0:T(8,128)} %bitcast.25), channel_id=1, replica_groups=mesh['grid'=64,'vec'=8] {'grid'}, dimensions={0} | all-to-all | bytes 4194304 | tf_op jit(solution)/shard_map/all_to_all | solution.py:29
  286.9 0.8 reduce_sum.18
  (36 shorter events, 2.1 us)
Async XLA Ops:
  6.5 129.8 %all-gather.3.cloned.1.call-start = ((), (), s32[]{:S(2)}) async-start(), calls=%async_computation.1 | async-start | bytes 12779520 | tf_op jit(solution)/shard_map/all_gather | solution.py:18
  9.2 202.2 %all-gather.5.cloned.1.call-start = ((), (), s32[]{:S(2)}) async-start(), calls=%async_computation.2 | async-start | bytes 3538944 | tf_op jit(solution)/shard_map/all_gather | solution.py:43
  143.6 10.0 %copy-start = (f32[3,128]{1,0:T(4,128)S(1)}, f32[3,128]{1,0:T(4,128)}, u32[]{:S(2)}) copy-start(f32[3,128]{1,0:T(4,128)} %param.6) | copy-start | bytes 4612
Sparse Core Ops, SparseCore 0:
  10.6 125.6 all-gather.2
  138.4 72.8 all-gather.4
where the time goes:
time: 296 us; the launch traced here: 294 us
  waiting for transfers between devices  146 us (49%)
  blocking collectives  66.6 us (22%)
  matrix products  39.9 us (13%)
  local copies, waits for them, and re-layouts  21 us (7%)
  between operations  13.4 us (5%)
  other arithmetic  6.7 us (2%)
    all_gather x1, waiting for transfers between devices, in_one_piece(): lax.all_gather(both, axis, axis=dim, tiled=True)  126 us
    all_to_all x1, blocking collectives, sum_at_owner(): lax.all_to_all(blocks, axis, split_axis=0, concat_axis=0, tiled=True)  66.6 us
    dot_general x16, matrix products, inner(): jnp.einsum('cts,qs->ctq', kern, vblock, precision=lax.Precision.HIGHEST)  32.8 us
    all_gather x1, waiting for transfers between devices, body(): gathered = lax.all_gather(grad_vectors, 'vec', axis=1, tiled=True)  18.9 us
    split x2, local copies, waits for them, and re-layouts, in_one_piece(): jnp.split(lax.all_gather(both, axis, axis=dim, tiled=True), ends, axis=al...  14.4 us
    dot_general x1, matrix products, body(): jnp.einsum('cpt,ctq->pq', gathered, total, precision=lax.Precision.HIGHEST)  7.14 us
  transfers between devices with their start and end apart: 2, of which 2 were waited for; matrix products, arithmetic and copies ran while one was open for 19% of the time, Pallas kernels for 0%

commit v1 on v0

v1 whole, which is shorter than its diff:
```python
import jax
import jax.numpy as jnp
from jax import lax
from jax.experimental import pallas as pl
from jax.experimental.pallas import tpu as pltpu
from jax.sharding import Mesh, PartitionSpec as P


SOFT2 = 0.05 * 0.05
TINY = 1e-30
GRID = ("yh", "y0", "h", "l", "c")
VEC = ("x", "zl")
SWAP = [(0, 1), (1, 0)]
BF16 = jnp.bfloat16


def copies(block, peers):
    return jnp.broadcast_to(block[None], (peers,) + block.shape)


def split(a):
    hi = a.astype(BF16)
    return hi, (a - hi.astype(jnp.float32)).astype(BF16)


def times_transposed(a, b):
    return lax.dot_general(a, b, (((1,), (1,)), ((), ())), preferred_element_type=jnp.float32)


def pair_matmul_kernel(origin_ref, own_ref, other_ref, src_ref, out_ref, hi_ref, lo_ref):
    blocks, _, half = own_ref.shape
    rows = out_ref.shape[1]
    origin = [origin_ref[comp : comp + 1, 0:1] for comp in range(3)]

    @pl.when(pl.program_id(0) == 0)
    def _():
        for j in range(blocks):
            for side, ref in enumerate((own_ref, other_ref)):
                cols = slice(side * half, (side + 1) * half)
                moment = None
                for comp in range(3):
                    g = ref[j, comp * rows : (comp + 1) * rows, :]
                    hi, lo = split(g)
                    hi_ref[j, (comp + 1) * rows : (comp + 2) * rows, cols] = hi
                    lo_ref[j, (comp + 1) * rows : (comp + 2) * rows, cols] = lo
                    tgt = ref[j, 3 * rows + comp : 3 * rows + comp + 1, :] - origin[comp]
                    moment = g * tgt if moment is None else moment + g * tgt
                hi, lo = split(moment)
                hi_ref[j, :rows, cols] = hi
                lo_ref[j, :rows, cols] = lo

    src = [src_ref[:, comp : comp + 1] for comp in range(3)]
    total = None
    for j in range(blocks):
        dist2 = None
        for comp in range(3):
            row = slice(3 * rows + comp, 3 * rows + comp + 1)
            tgt = jnp.concatenate([own_ref[j, row, :], other_ref[j, row, :]], axis=1)
            diff = tgt - src[comp]
            dist2 = diff * diff if dist2 is None else dist2 + diff * diff
        grow = 1.0 + dist2 * lax.rsqrt(jnp.maximum(dist2, TINY))
        grow2 = grow * grow
        hi, lo = split(lax.rsqrt((dist2 + SOFT2) * (grow2 * grow2)))
        part = times_transposed(hi, hi_ref[j]) + times_transposed(lo, hi_ref[j]) + times_transposed(hi, lo_ref[j])
        total = part if total is None else total + part
    z = total[:, :rows]
    for comp in range(3):
        z = z - (src[comp] - origin[comp]) * total[:, (comp + 1) * rows : (comp + 2) * rows]
    out_ref[0] = (0.5 * z).T


def pair_matmul(origin, own, other, src_cols, peers):
    blocks, height, half = own.shape
    rows = (height - 8) // 3
    total_s = src_cols.shape[0]
    per = total_s // peers
    step = 512
    inner = per // step
    pairs = total_s * 2 * half * blocks
    return pl.pallas_call(
        pair_matmul_kernel,
        out_shape=jax.ShapeDtypeStruct((peers, rows, per), jnp.float32),
        grid=(total_s // step,),
        in_specs=[
            pl.BlockSpec((8, half), lambda i: (0, 0)),
            pl.BlockSpec((blocks, height, half), lambda i: (0, 0, 0)),
            pl.BlockSpec((blocks, height, half), lambda i: (0, 0, 0)),
            pl.BlockSpec((step, 8), lambda i: (i, 0)),
        ],
        out_specs=pl.BlockSpec((1, rows, step), lambda i: (i // inner, 0, i % inner)),
        scratch_shapes=[pltpu.VMEM((blocks, 4 * rows, 2 * half), BF16)] * 2,
        compiler_params=pltpu.CompilerParams(
            dimension_semantics=("arbitrary",), vmem_limit_bytes=32 * 1024 * 1024
        ),
        cost_estimate=pl.CostEstimate(
            flops=pairs * 4 * rows * 2 * 3,
            bytes_accessed=2 * blocks * height * half * 4 + peers * rows * per * 4,
            transcendentals=2 * pairs,
        ),
    )(origin, own, other, src_cols)


def body(tgt_coords, src_coords, src_values, grad_vectors):
    n = {a: lax.axis_size(a) for a in GRID + VEC}
    nv = n["x"] * n["zl"]
    slab, pts = src_values.shape
    rows = slab // n["h"]
    zrows = rows // n["l"]
    piece = zrows // n["c"]
    h = lax.axis_index("h")
    c = lax.axis_index("c")

    grads = grad_vectors.reshape(3, n["h"], rows, pts)
    tail = jnp.concatenate([tgt_coords, jnp.zeros((5, pts), jnp.float32)], axis=0)
    first, second = (jnp.concatenate([grads[:, k].reshape(3 * rows, pts), tail], axis=0) for k in range(2))
    mine = jnp.where(h == 0, first, second)
    theirs = jnp.where(h == 0, second, first)
    from_z = lax.ppermute(theirs, "h", SWAP)
    from_diag = lax.ppermute(theirs, ("y0", "h"), [(i, 3 - i) for i in range(4)])
    from_y = lax.ppermute(mine, "y0", SWAP)

    src_pad = jnp.concatenate([src_coords, jnp.zeros((5, pts), jnp.float32)], axis=0)
    nsrc = n["yh"] * n["h"] * n["l"]
    src_all = lax.all_to_all(copies(src_pad, nsrc), ("yh", "h", "l"), 0, 0, tiled=True)
    src_cols = src_all.transpose(0, 2, 1).reshape(nsrc * pts, 8)
    origin = jnp.broadcast_to(jnp.mean(src_all, axis=(0, 2))[:, None], (8, pts))

    own = jnp.stack([mine, from_y, from_z, from_diag])
    other = lax.ppermute(own, "c", SWAP)

    partial_z = pair_matmul(origin, own, other, src_cols, n["yh"])
    src_values, partial_z = lax.optimization_barrier((src_values, partial_z))

    spts = partial_z.shape[2]
    arrived = lax.all_to_all(
        partial_z.reshape(n["yh"] * n["l"], zrows, spts), ("yh", "l"), 0, 0, tiled=True
    )
    v_l = lax.ppermute(src_values, "l", SWAP)
    v_h = lax.ppermute(src_values, "h", SWAP)
    v_hl = lax.ppermute(src_values, ("h", "l"), [(i, 3 - i) for i in range(4)])
    me = lax.axis_index(("h", "l"))
    stack = jnp.stack([src_values, v_l, v_h, v_hl])
    values = jnp.concatenate([lax.dynamic_index_in_dim(stack, me ^ b, 0, False) for b in range(4)], axis=1)

    z = arrived.sum(axis=0)
    z_all = lax.all_to_all(copies(z, nv), VEC, 0, 0, tiled=True).reshape(nv, n["c"], piece, spts)

    def product(core):
        zc = lax.dynamic_index_in_dim(z_all, core, 1, False).reshape(nv * piece, spts)
        return lax.dot_general(zc, values, (((1,), (1,)), ((), ())), precision=lax.Precision.HIGH)

    part = lax.ppermute(product(1 - c), "c", SWAP) + product(c)
    back = lax.all_to_all(part.reshape(nv, piece, slab), ("yh", "y0"), 0, 0, tiled=True)
    return back.sum(axis=0)


def solution(mesh):
    fine = Mesh(mesh.devices.reshape(4, 2, 2, 2, 2, 4, 2), GRID + VEC)

    return jax.shard_map(
        body,
        mesh=fine,
        in_specs=(P(None, GRID), P(None, GRID), P(VEC, GRID), P(None, VEC, GRID)),
        out_specs=P(GRID, VEC),
        check_vma=False,
    )
```

time: 296 us -> 153 us (0.52)
  the two profiles are of different devices: /device:TPU:24 before, /device:TPU:2 now
where the time goes in v1:
time: 153 us; the launch traced here: 152 us
  blocking collectives  73.2 us (48%)
  starting transfers between devices  38.1 us (25%)
  waiting for transfers between devices  24.9 us (16%)
  Pallas kernels  10.2 us (7%)
  local copies, waits for them, and re-layouts  3.46 us (2%)
    all_to_all x1, blocking collectives, body(): lax.all_to_all(partial_z.reshape(n['yh'] * n['l'], zrows, spts), ('yh', '...  32.7 us
    all_to_all x1, blocking collectives, body(): lax.all_to_all(copies(src_pad, nsrc), ('yh', 'h', 'l'), 0, 0, tiled=True)  24.6 us
    all_to_all x1, blocking collectives, body(): lax.all_to_all(part.reshape(nv, piece, slab), ('yh', 'y0'), 0, 0, tiled=T...  15.9 us
    ppermute x1, starting transfers between devices, body(): from_z = lax.ppermute(theirs, 'h', SWAP)  10.9 us
    pallas_call x1, Pallas kernels, pair_matmul(): pl.pallas_call(pair_matmul_kernel, out_shape=jax.ShapeDtypeStruct((peers,...  10.2 us
    ppermute x1, waiting for transfers between devices, body(): from_z = lax.ppermute(theirs, 'h', SWAP)  9.44 us
    ppermute x1, waiting for transfers between devices, body(): v_l = lax.ppermute(src_values, 'l', SWAP)  8.21 us
    ppermute x1, starting transfers between devices, body(): v_hl = lax.ppermute(src_values, ('h', 'l'), [(i, 3 - i) for i in range(4)])  7.08 us
  transfers between devices with their start and end apart: 9, of which 5 were waited for; matrix products, arithmetic and copies ran while one was open for 0% of the time, Pallas kernels for 0%

profile of v1, /device:TPU:2, one launch (start us, length us, event | category | flops | bytes accessed | tf_op | source)
XLA Modules:
  0.0 152.0 jit_solution(3416788876855634230)
XLA Ops:
  0.0 1.0 fusion.10
  1.1 0.1 pad.24.clone
  1.1 0.0 copy-start.1
  1.1 0.7 copy-done.1
  1.8 0.1 fusion.7
  1.9 10.9 %collective-permute-start.1 = (f32[392,128]{1,0:T(8,128)S(1)}, f32[392,128]{1,0:T(8,128)S(1)}, u32[]{:S(2)}, u32[]{:S(2)}) collective-permute-start(f32[392,128]{1,0:T(8,128)S(1)} %get-tuple-element.16), channel_id=1, source_target_pairs={{0,32},{32,0},{1,33},{33,1},{2,34},{34,2},{3,35},{35,3},{4,36},{36... | collective-permute-start | bytes 602120 | tf_op jit(solution)/shard_map/ppermute | solution.py:118
  12.9 2.9 %collective-permute-start.2 = (f32[392,128]{1,0:T(8,128)S(1)}, f32[392,128]{1,0:T(8,128)S(1)}, u32[]{:S(2)}, u32[]{:S(2)}) collective-permute-start(f32[392,128]{1,0:T(8,128)S(1)} %get-tuple-element.16), channel_id=1, source_target_pairs={{0,96},{32,64},{64,32},{96,0},{1,97},{33,65},{65,33},{97,1},{2,98}... | collective-permute-start | bytes 602120 | tf_op jit(solution)/shard_map/ppermute | solution.py:119
  15.8 2.5 %collective-permute-start = (f32[392,128]{1,0:T(8,128)S(1)}, f32[392,128]{1,0:T(8,128)S(1)}, u32[]{:S(2)}, u32[]{:S(2)}) collective-permute-start(f32[392,128]{1,0:T(8,128)S(1)} %get-tuple-element.15), channel_id=1, source_target_pairs={{0,64},{64,0},{1,65},{65,1},{2,66},{66,2},{3,67},{67,3},{4,68},{68... | collective-permute-start | bytes 602120 | tf_op jit(solution)/shard_map/ppermute | solution.py:120
  18.3 0.1 fusion.4
  18.4 9.4 %collective-permute-done.1 = f32[392,128]{1,0:T(8,128)S(1)} collective-permute-done((f32[392,128]{1,0:T(8,128)S(1)}, f32[392,128]{1,0:T(8,128)S(1)}, u32[]{:S(2)}, u32[]{:S(2)}) %collective-permute-start.1) | collective-permute-done | bytes 200736 | tf_op jit(solution)/shard_map/ppermute | solution.py:118
  27.9 2.9 %collective-permute-done.2 = f32[392,128]{1,0:T(8,128)S(1)} collective-permute-done((f32[392,128]{1,0:T(8,128)S(1)}, f32[392,128]{1,0:T(8,128)S(1)}, u32[]{:S(2)}, u32[]{:S(2)}) %collective-permute-start.2) | collective-permute-done | bytes 200736 | tf_op jit(solution)/shard_map/ppermute | solution.py:119
  30.7 0.0 collective-permute-done
  30.7 0.0 copy-start.2
  30.7 0.1 pad_maximum_fusion.own_ref
  30.8 1.9 %collective-permute-start.3 = (f32[4,392,128]{2,1,0:T(8,128)S(1)}, f32[4,392,128]{2,1,0:T(8,128)S(1)}, u32[]{:S(2)}, u32[]{:S(2)}) collective-permute-start(f32[4,392,128]{2,1,0:T(8,128)S(1)} %pad_maximum_fusion.own_ref), channel_id=1, source_target_pairs={{0,8},{8,0},{1,9},{9,1},{2,10},{10,2},{3,11},{11,3},{4,12},{12,4},... | collective-permute-start | bytes 2408456 | tf_op jit(solution)/shard_map/ppermute | solution.py:129
  32.8 0.0 copy-done.2
  32.8 24.6 %all_to_all.20 = f32[16,8,128]{2,1,0:T(8,128)S(1)} all-to-all(f32[16,8,128]{2,1,0:T(8,128)S(1)} %broadcast_in_dim.6), channel_id=1, replica_groups=mesh['yh'=4,'y0'=2,'h'=2,'l'=2,'c'=2,'x'=4,'zl'=2] {'yh','h','l'}, dimensions={0} | all-to-all | bytes 131072 | tf_op jit(solution)/shard_map/all_to_all | solution.py:124
  57.4 0.3 copy.10
  57.7 0.1 reduce_sum.27
  57.8 0.0 collective-permute-done.3.other_ref
  57.8 0.1 broadcast_in_dim.7.origin_ref
  57.9 10.2 %shard_map.46 = f32[4,128,512]{2,1,0:T(8,128)S(1)} custom-call(f32[8,128]{1,0:T(8,128)S(1)} %broadcast_in_dim.7.origin_ref, f32[4,392,128]{2,1,0:T(8,128)S(1)} %pad_maximum_fusion.own_ref, f32[4,392,128]{2,1,0:T(8,128)S(1)} %collective-permute-done.3.other_ref, f32[2048,8]{1,0:T(8,128)S(1)} %bitcast.36), custom_call_target="tpu_custom_call" | custom-call | flops 6442450944 | bytes 2654208 | tf_op jit(solution)/shard_map/pallas_call | solution.py:80
  68.1 32.7 %all_to_all.21 = f32[8,64,512]{2,1,0:T(8,128)S(1)} all-to-all(f32[8,64,512]{2,1,0:T(8,128)S(1)} %bitcast.37), channel_id=1, replica_groups=mesh['yh'=4,'y0'=2,'h'=2,'l'=2,'c'=2,'x'=4,'zl'=2] {'yh','l'}, dimensions={0} | all-to-all | bytes 2097152 | tf_op jit(solution)/shard_map/all_to_all | solution.py:135
  100.8 0.1 reduce_sum.28
  100.9 1.1 broadcast_in_dim.8
  102.0 0.0 copy-start
  102.0 5.7 %all-to-all-start.2 = ((f32[8,64,512]{2,1,0:T(8,128)}), f32[8,64,512]{2,1,0:T(8,128)S(1)}, u32[]{:S(2)}, u32[]{:S(2)}) async-start(f32[8,64,512]{2,1,0:T(8,128)} %broadcast_in_dim.8), calls=%async_computation.2 | async-start | bytes 2097152 | tf_op jit(solution)/shard_map/all_to_all | solution.py:146
  107.7 0.0 copy-done
  107.7 1.9 %collective-permute-start.4 = (f32[256,128]{1,0:T(8,128)S(1)}, f32[256,128]{1,0:T(8,128)S(1)}, u32[]{:S(2)}, u32[]{:S(2)}) collective-permute-start(f32[256,128]{1,0:T(8,128)S(1)} %copy-done), channel_id=1, source_target_pairs={{0,16},{16,0},{1,17},{17,1},{2,18},{18,2},{3,19},{19,3},{4,20},{20... | collective-permute-start | bytes 393224 | tf_op jit(solution)/shard_map/ppermute | solution.py:138
  109.6 3.2 %collective-permute-start.5 = (f32[256,128]{1,0:T(8,128)S(1)}, f32[256,128]{1,0:T(8,128)S(1)}, u32[]{:S(2)}, u32[]{:S(2)}) collective-permute-start(f32[256,128]{1,0:T(8,128)S(1)} %copy-done), channel_id=1, source_target_pairs={{0,32},{32,0},{1,33},{33,1},{2,34},{34,2},{3,35},{35,3},{4,36},{36... | collective-permute-start | bytes 393224 | tf_op jit(solution)/shard_map/ppermute | solution.py:139
  112.9 7.1 %collective-permute-start.6 = (f32[256,128]{1,0:T(8,128)S(1)}, f32[256,128]{1,0:T(8,128)S(1)}, u32[]{:S(2)}, u32[]{:S(2)}) collective-permute-start(f32[256,128]{1,0:T(8,128)S(1)} %copy-done), channel_id=1, source_target_pairs={{0,48},{16,32},{32,16},{48,0},{1,49},{17,33},{33,17},{49,1},{2,50}... | collective-permute-start | bytes 393224 | tf_op jit(solution)/shard_map/ppermute | solution.py:140
  120.0 8.2 %collective-permute-done.4 = f32[256,128]{1,0:T(8,128)S(1)} collective-permute-done((f32[256,128]{1,0:T(8,128)S(1)}, f32[256,128]{1,0:T(8,128)S(1)}, u32[]{:S(2)}, u32[]{:S(2)}) %collective-permute-start.4) | collective-permute-done | bytes 131104 | tf_op jit(solution)/shard_map/ppermute | solution.py:138
  128.2 2.8 %collective-permute-done.5 = f32[256,128]{1,0:T(8,128)S(1)} collective-permute-done((f32[256,128]{1,0:T(8,128)S(1)}, f32[256,128]{1,0:T(8,128)S(1)}, u32[]{:S(2)}, u32[]{:S(2)}) %collective-permute-start.5) | collective-permute-done | bytes 131104 | tf_op jit(solution)/shard_map/ppermute | solution.py:139
  131.0 0.0 collective-permute-done.6
  131.1 0.0 all-to-all-done.2
  131.1 0.1 constant_dynamic-slice_fusion
  131.2 0.4 fusion
  131.7 1.9 %collective-permute-start.7 = (f32[256,256]{1,0:T(8,128)S(1)}, f32[256,256]{1,0:T(8,128)S(1)}, u32[]{:S(2)}, u32[]{:S(2)}) collective-permute-start(f32[256,256]{1,0:T(8,128)S(1)} %fusion), channel_id=1, source_target_pairs={{0,8},{8,0},{1,9},{9,1},{2,10},{10,2},{3,11},{11,3},{4,12},{12,4},... | collective-permute-start | bytes 786440 | tf_op jit(solution)/shard_map/ppermute | solution.py:152
  133.6 1.5 collective-permute-done.7
  135.1 0.4 convolution_add_fusion
  135.5 15.9 %all_to_all.22 = f32[8,32,256]{2,1,0:T(8,128)S(1)} all-to-all(f32[8,32,256]{2,1,0:T(8,128)S(1)} %bitcast.45), channel_id=1, replica_groups=mesh['yh'=4,'y0'=2,'h'=2,'l'=2,'c'=2,'x'=4,'zl'=2] {'yh','y0'}, dimensions={0} | all-to-all | bytes 524288 | tf_op jit(solution)/shard_map/all_to_all | solution.py:153
  151.4 0.6 reduce_sum.29
  (6 shorter events, 0.1 us)
Async XLA Ops:
  1.1 0.7 copy-start.1
  1.9 25.9 %collective-permute-start.1 = (f32[392,128]{1,0:T(8,128)S(1)}, f32[392,128]{1,0:T(8,128)S(1)}, u32[]{:S(2)}, u32[]{:S(2)}) collective-permute-start(f32[392,128]{1,0:T(8,128)S(1)} %get-tuple-element.16), channel_id=1, source_target_pairs={{0,32},{32,0},{1,33},{33,1},{2,34},{34,2},{3,35},{35,3},{4,36},{36... | collective-permute-start | bytes 602120 | tf_op jit(solution)/shard_map/ppermute | solution.py:118
  12.9 17.9 %collective-permute-start.2 = (f32[392,128]{1,0:T(8,128)S(1)}, f32[392,128]{1,0:T(8,128)S(1)}, u32[]{:S(2)}, u32[]{:S(2)}) collective-permute-start(f32[392,128]{1,0:T(8,128)S(1)} %get-tuple-element.16), channel_id=1, source_target_pairs={{0,96},{32,64},{64,32},{96,0},{1,97},{33,65},{65,33},{97,1},{2,98}... | collective-permute-start | bytes 602120 | tf_op jit(solution)/shard_map/ppermute | solution.py:119
  15.8 14.9 %collective-permute-start = (f32[392,128]{1,0:T(8,128)S(1)}, f32[392,128]{1,0:T(8,128)S(1)}, u32[]{:S(2)}, u32[]{:S(2)}) collective-permute-start(f32[392,128]{1,0:T(8,128)S(1)} %get-tuple-element.15), channel_id=1, source_target_pairs={{0,64},{64,0},{1,65},{65,1},{2,66},{66,2},{3,67},{67,3},{4,68},{68... | collective-permute-start | bytes 602120 | tf_op jit(solution)/shard_map/ppermute | solution.py:120
  30.7 2.0 %copy-start.2 = (f32[3,128]{1,0:T(4,128)S(1)}, f32[3,128]{1,0:T(4,128)}, u32[]{:S(2)}) copy-start(f32[3,128]{1,0:T(4,128)} %param.5) | copy-start | bytes 4612
  30.8 27.0 %collective-permute-start.3 = (f32[4,392,128]{2,1,0:T(8,128)S(1)}, f32[4,392,128]{2,1,0:T(8,128)S(1)}, u32[]{:S(2)}, u32[]{:S(2)}) collective-permute-start(f32[4,392,128]{2,1,0:T(8,128)S(1)} %pad_maximum_fusion.own_ref), channel_id=1, source_target_pairs={{0,8},{8,0},{1,9},{9,1},{2,10},{10,2},{3,11},{11,3},{4,12},{12,4},... | collective-permute-start | bytes 2408456 | tf_op jit(solution)/shard_map/ppermute | solution.py:129
  102.0 5.7 %copy-start = (f32[256,128]{1,0:T(8,128)S(1)}, f32[256,128]{1,0:T(8,128)}, u32[]{:S(2)}) copy-start(f32[256,128]{1,0:T(8,128)} %param.6) | copy-start | bytes 393220
  102.0 29.1 %all-to-all-start.2 = ((f32[8,64,512]{2,1,0:T(8,128)}), f32[8,64,512]{2,1,0:T(8,128)S(1)}, u32[]{:S(2)}, u32[]{:S(2)}) async-start(f32[8,64,512]{2,1,0:T(8,128)} %broadcast_in_dim.8), calls=%async_computation.2 | async-start | bytes 2097152 | tf_op jit(solution)/shard_map/all_to_all | solution.py:146
  107.7 20.5 %collective-permute-start.4 = (f32[256,128]{1,0:T(8,128)S(1)}, f32[256,128]{1,0:T(8,128)S(1)}, u32[]{:S(2)}, u32[]{:S(2)}) collective-permute-start(f32[256,128]{1,0:T(8,128)S(1)} %copy-done), channel_id=1, source_target_pairs={{0,16},{16,0},{1,17},{17,1},{2,18},{18,2},{3,19},{19,3},{4,20},{20... | collective-permute-start | bytes 393224 | tf_op jit(solution)/shard_map/ppermute | solution.py:138
  109.6 21.4 %collective-permute-start.5 = (f32[256,128]{1,0:T(8,128)S(1)}, f32[256,128]{1,0:T(8,128)S(1)}, u32[]{:S(2)}, u32[]{:S(2)}) collective-permute-start(f32[256,128]{1,0:T(8,128)S(1)} %copy-done), channel_id=1, source_target_pairs={{0,32},{32,0},{1,33},{33,1},{2,34},{34,2},{3,35},{35,3},{4,36},{36... | collective-permute-start | bytes 393224 | tf_op jit(solution)/shard_map/ppermute | solution.py:139
  112.9 18.2 %collective-permute-start.6 = (f32[256,128]{1,0:T(8,128)S(1)}, f32[256,128]{1,0:T(8,128)S(1)}, u32[]{:S(2)}, u32[]{:S(2)}) collective-permute-start(f32[256,128]{1,0:T(8,128)S(1)} %copy-done), channel_id=1, source_target_pairs={{0,48},{16,32},{32,16},{48,0},{1,49},{17,33},{33,17},{49,1},{2,50}... | collective-permute-start | bytes 393224 | tf_op jit(solution)/shard_map/ppermute | solution.py:140
  131.7 3.4 %collective-permute-start.7 = (f32[256,256]{1,0:T(8,128)S(1)}, f32[256,256]{1,0:T(8,128)S(1)}, u32[]{:S(2)}, u32[]{:S(2)}) collective-permute-start(f32[256,256]{1,0:T(8,128)S(1)} %fusion), channel_id=1, source_target_pairs={{0,8},{8,0},{1,9},{9,1},{2,10},{10,2},{3,11},{11,3},{4,12},{12,4},... | collective-permute-start | bytes 786440 | tf_op jit(solution)/shard_map/ppermute | solution.py:152

commit v2 on v1

--- a/solution.py
+++ b/solution.py
@@ -12,6 +12,7 @@
 VEC = ("x", "zl")
 SWAP = [(0, 1), (1, 0)]
 BF16 = jnp.bfloat16
+TAIL = 8
 
 
 def copies(block, peers):
@@ -71,10 +72,10 @@
 
 def pair_matmul(origin, own, other, src_cols, peers):
     blocks, height, half = own.shape
-    rows = (height - 8) // 3
+    rows = (height - TAIL) // 3
     total_s = src_cols.shape[0]
     per = total_s // peers
-    step = 512
+    step = STEP
     inner = per // step
     pairs = total_s * 2 * half * blocks
     return pl.pallas_call(
@@ -100,50 +101,46 @@
     )(origin, own, other, src_cols)
 
 
+STEP = 512
+
+
 def body(tgt_coords, src_coords, src_values, grad_vectors):
     n = {a: lax.axis_size(a) for a in GRID + VEC}
+    nz = n["h"] * n["l"]
     nv = n["x"] * n["zl"]
     slab, pts = src_values.shape
-    rows = slab // n["h"]
-    zrows = rows // n["l"]
-    piece = zrows // n["c"]
-    h = lax.axis_index("h")
+    rows = slab // nz
+    piece = rows // n["c"]
     c = lax.axis_index("c")
 
-    grads = grad_vectors.reshape(3, n["h"], rows, pts)
-    tail = jnp.concatenate([tgt_coords, jnp.zeros((5, pts), jnp.float32)], axis=0)
-    first, second = (jnp.concatenate([grads[:, k].reshape(3 * rows, pts), tail], axis=0) for k in range(2))
-    mine = jnp.where(h == 0, first, second)
-    theirs = jnp.where(h == 0, second, first)
-    from_z = lax.ppermute(theirs, "h", SWAP)
-    from_diag = lax.ppermute(theirs, ("y0", "h"), [(i, 3 - i) for i in range(4)])
-    from_y = lax.ppermute(mine, "y0", SWAP)
-
-    src_pad = jnp.concatenate([src_coords, jnp.zeros((5, pts), jnp.float32)], axis=0)
-    nsrc = n["yh"] * n["h"] * n["l"]
-    src_all = lax.all_to_all(copies(src_pad, nsrc), ("yh", "h", "l"), 0, 0, tiled=True)
-    src_cols = src_all.transpose(0, 2, 1).reshape(nsrc * pts, 8)
-    origin = jnp.broadcast_to(jnp.mean(src_all, axis=(0, 2))[:, None], (8, pts))
-
-    own = jnp.stack([mine, from_y, from_z, from_diag])
+    grads = grad_vectors.reshape(3, nz, rows, pts).transpose(1, 0, 2, 3).reshape(nz, 3 * rows, pts)
+    tail = jnp.concatenate([tgt_coords, src_coords, jnp.zeros((TAIL - 6, pts), jnp.float32)], axis=0)
+    load = jnp.concatenate([grads, copies(tail, nz)], axis=1)
+    load = copies(load, n["y0"]).reshape(n["y0"] * nz, 3 * rows + TAIL, pts)
+    own = lax.all_to_all(load, ("y0", "h", "l"), 0, 0, tiled=True)
     other = lax.ppermute(own, "c", SWAP)
 
+    near = own[:, 3 * rows + 3 : 3 * rows + 6, :].reshape(n["y0"], 3 * nz, pts)
+    near = lax.dynamic_index_in_dim(near, lax.axis_index("y0"), 0, False)
+    near = jnp.pad(near, ((0, 4), (0, 0)))
+    src_all = lax.all_to_all(copies(near, n["yh"]), "yh", 0, 0, tiled=True)
+    src_all = src_all[:, : 3 * nz].reshape(n["yh"] * nz, 3, pts)
+    src_cols = src_all.transpose(0, 2, 1).reshape(n["yh"] * nz * pts, 3)
+    src_cols = jnp.pad(src_cols, ((0, 0), (0, 5)))
+    origin = jnp.mean(src_all, axis=(0, 2))
+    origin = jnp.broadcast_to(jnp.pad(origin, (0, 5))[:, None], (8, pts))
+    src_values, src_cols = lax.optimization_barrier((src_values, src_cols))
+
+    values = lax.all_to_all(copies(src_values, nz), ("h", "l"), 0, 0, tiled=True)
+
     partial_z = pair_matmul(origin, own, other, src_cols, n["yh"])
-    src_values, partial_z = lax.optimization_barrier((src_values, partial_z))
+    spts = partial_z.shape[2]
+    partial_z, values = lax.optimization_barrier((partial_z, values))
 
-    spts = partial_z.shape[2]
-    arrived = lax.all_to_all(
-        partial_z.reshape(n["yh"] * n["l"], zrows, spts), ("yh", "l"), 0, 0, tiled=True
-    )
-    v_l = lax.ppermute(src_values, "l", SWAP)
-    v_h = lax.ppermute(src_values, "h", SWAP)
-    v_hl = lax.ppermute(src_values, ("h", "l"), [(i, 3 - i) for i in range(4)])
-    me = lax.axis_index(("h", "l"))
-    stack = jnp.stack([src_values, v_l, v_h, v_hl])
-    values = jnp.concatenate([lax.dynamic_index_in_dim(stack, me ^ b, 0, False) for b in range(4)], axis=1)
-
+    arrived = lax.all_to_all(partial_z, "yh", 0, 0, tiled=True)
     z = arrived.sum(axis=0)
     z_all = lax.all_to_all(copies(z, nv), VEC, 0, 0, tiled=True).reshape(nv, n["c"], piece, spts)
+    values = values.transpose(1, 0, 2).reshape(slab, spts)
 
     def product(core):
         zc = lax.dynamic_index_in_dim(z_all, core, 1, False).reshape(nv * piece, spts)

time: 153 us -> 137 us (0.90)
  the two profiles are of different devices: /device:TPU:2 before, /device:TPU:1 now
where the time goes in v2:
time: 137 us; the launch traced here: 136 us
  blocking collectives  77.8 us (57%)
  starting transfers between devices  21.3 us (16%)
  Pallas kernels  14.5 us (11%)
  waiting for transfers between devices  11.9 us (9%)
  local copies, waits for them, and re-layouts  6.79 us (5%)
  matrix products  2.85 us (2%)
    all_to_all x1, blocking collectives, body(): own = lax.all_to_all(load, ('y0', 'h', 'l'), 0, 0, tiled=True)  33.9 us
    all_to_all x1, blocking collectives, body(): lax.all_to_all(part.reshape(nv, piece, slab), ('yh', 'y0'), 0, 0, tiled=T...  15.9 us
    all_to_all x1, blocking collectives, body(): arrived = lax.all_to_all(partial_z, 'yh', 0, 0, tiled=True)  15.4 us
    pallas_call x1, Pallas kernels, pair_matmul(): pl.pallas_call(pair_matmul_kernel, out_shape=jax.ShapeDtypeStruct((peers,...  14.5 us
    all_to_all x1, blocking collectives, body(): src_all = lax.all_to_all(copies(near, n['yh']), 'yh', 0, 0, tiled=True)  12.6 us
    all_to_all x1, waiting for transfers between devices, body(): lax.all_to_all(copies(z, nv), VEC, 0, 0, tiled=True)  10.5 us
    ppermute x1, starting transfers between devices, body(): part = lax.ppermute(product(1 - c), 'c', SWAP) + product(c)  8.84 us
    ppermute x1, starting transfers between devices, body(): other = lax.ppermute(own, 'c', SWAP)  4.35 us
  transfers between devices with their start and end apart: 4, of which 3 were waited for; matrix products, arithmetic and copies ran while one was open for 3% of the time, Pallas kernels for 11%

profile of v2, /device:TPU:1, one launch (start us, length us, event | category | flops | bytes accessed | tf_op | source)
XLA Modules:
  0.0 136.2 jit_solution(3172451546869008157)
XLA Ops:
  0.0 0.0 copy-start.2
  0.0 1.0 copy.7
  1.0 0.0 copy-start.1
  1.1 0.1 pad.19.clone
  1.1 0.0 copy-done.2
  1.1 0.6 copy-done.1
  1.7 0.1 maximum_maximum_fusion
  1.8 0.1 broadcast_in_dim.16
  1.9 33.9 %all_to_all.30.own_ref = f32[8,200,128]{2,1,0:T(8,128)S(1)} all-to-all(f32[8,200,128]{2,1,0:T(8,128)S(1)} %bitcast.22), channel_id=1, replica_groups=mesh['yh'=4,'y0'=2,'h'=2,'l'=2,'c'=2,'x'=4,'zl'=2] {'y0','h','l'}, dimensions={0} | all-to-all | bytes 1638400 | tf_op jit(solution)/shard_map/all_to_all | solution.py:120
  35.8 4.3 %collective-permute-start = (f32[8,200,128]{2,1,0:T(8,128)S(1)}, f32[8,200,128]{2,1,0:T(8,128)S(1)}, u32[]{:S(2)}, u32[]{:S(2)}) collective-permute-start(f32[8,200,128]{2,1,0:T(8,128)S(1)} %all_to_all.30.own_ref), channel_id=1, source_target_pairs={{0,8},{8,0},{1,9},{9,1},{2,10},{10,2},{3,11},{11,3},{4,12},{12,4},... | collective-permute-start | bytes 2457608 | tf_op jit(solution)/shard_map/ppermute | solution.py:121
  40.3 12.6 %all_to_all.31 = f32[4,16,128]{2,1,0:T(8,128)S(1)} all-to-all(f32[4,16,128]{2,1,0:T(8,128)S(1)} %broadcast_in_dim.17), channel_id=1, replica_groups=mesh['yh'=4,'y0'=2,'h'=2,'l'=2,'c'=2,'x'=4,'zl'=2] {'yh'}, dimensions={0} | all-to-all | bytes 65536 | tf_op jit(solution)/shard_map/all_to_all | solution.py:126
  52.8 0.1 fusion
  52.9 1.4 copy.8
  54.3 0.0 copy-start
  54.3 1.3 pad.14.src_ref
  55.6 0.1 reduce_sum.35
  55.7 0.0 copy-done
  55.7 0.1 copy.9
  55.8 0.8 broadcast_in_dim.19
  56.7 4.1 %all-to-all-start.2 = ((f32[4,256,128]{1,2,0:T(8,128)}), f32[4,256,128]{1,2,0:T(8,128)}, u32[]{:S(2)}, u32[]{:S(2)}) async-start(f32[4,256,128]{1,2,0:T(8,128)} %broadcast_in_dim.19), calls=%async_computation.2 | async-start | bytes 1048576 | tf_op jit(solution)/shard_map/all_to_all | solution.py:134
  60.8 0.0 collective-permute-done.other_ref
  60.8 0.1 broadcast_in_dim.18.origin_ref
  60.9 14.5 %shard_map.46 = f32[4,64,512]{2,1,0:T(8,128)S(1)} custom-call(f32[8,128]{1,0:T(8,128)S(1)} %broadcast_in_dim.18.origin_ref, f32[8,200,128]{2,1,0:T(8,128)S(1)} %all_to_all.30.own_ref, f32[8,200,128]{2,1,0:T(8,128)S(1)} %collective-permute-done.other_ref, f32[2048,8]{1,0:T(8,128)S(1)} %pad.14.src_ref), custom_call_target="tpu_custom_call" | custom-call | flops 6442450944 | bytes 2162688 | tf_op jit(solution)/shard_map/pallas_call | solution.py:81
  75.4 0.3 all-to-all-done.2
  75.7 15.4 %all_to_all.32 = f32[4,64,512]{2,1,0:T(8,128)S(1)} all-to-all(f32[4,64,512]{2,1,0:T(8,128)S(1)} %shard_map.46), channel_id=1, replica_groups=mesh['yh'=4,'y0'=2,'h'=2,'l'=2,'c'=2,'x'=4,'zl'=2] {'yh'}, dimensions={0} | all-to-all | bytes 1048576 | tf_op jit(solution)/shard_map/all_to_all | solution.py:140
  91.2 1.1 broadcast_in_dim.20
  92.3 4.0 %all-to-all-start.4 = ((f32[8,64,512]{2,1,0:T(8,128)}), f32[8,64,512]{2,1,0:T(8,128)S(1)}, u32[]{:S(2)}, u32[]{:S(2)}) async-start(f32[8,64,512]{2,1,0:T(8,128)} %broadcast_in_dim.20), calls=%async_computation.4 | async-start | bytes 2097152 | tf_op jit(solution)/shard_map/all_to_all | solution.py:142
  96.3 10.5 %all-to-all-done.4 = f32[8,64,512]{2,1,0:T(8,128)S(1)} async-done(((f32[8,64,512]{2,1,0:T(8,128)}), f32[8,64,512]{2,1,0:T(8,128)S(1)}, u32[]{:S(2)}, u32[]{:S(2)}) %all-to-all-start.4) | async-done | bytes 1048608 | tf_op jit(solution)/shard_map/all_to_all | solution.py:142
  106.8 0.1 constant_dynamic-slice_fusion
  106.9 1.4 %fusion.1 = f32[256,256]{1,0:T(8,128)S(1)} fusion(f32[256,512]{1,0:T(8,128)S(1)} %bitcast.24, f32[256,512]{0,1:T(8,128)} %bitcast.10), kind=kOutput, calls=%fused_computation.9 | convolution fusion | flops 201326592 | bytes 1310720 | tf_op jit(solution)/shard_map/dot_general | solution.py:147
  108.3 8.8 %collective-permute-start.1 = (f32[256,256]{1,0:T(8,128)S(1)}, f32[256,256]{1,0:T(8,128)S(1)}, u32[]{:S(2)}, u32[]{:S(2)}) collective-permute-start(f32[256,256]{1,0:T(8,128)S(1)} %fusion.1), channel_id=1, source_target_pairs={{0,8},{8,0},{1,9},{9,1},{2,10},{10,2},{3,11},{11,3},{4,12},{12,4},... | collective-permute-start | bytes 786440 | tf_op jit(solution)/shard_map/ppermute | solution.py:149
  117.2 1.1 collective-permute-done.1
  118.3 1.4 %convolution_add_fusion = f32[256,256]{1,0:T(8,128)S(1)} fusion(f32[256,256]{1,0:T(8,128)S(1)} %collective-permute-done.1, f32[256,512]{1,0:T(8,128)S(1)} %bitcast.23, f32[256,512]{0,1:T(8,128)} %bitcast.10), kind=kOutput, calls=%fused_computation | convolution fusion | flops 201392128 | bytes 1572864 | tf_op jit(solution)/shard_map/dot_general | solution.py:147
  119.7 15.9 %all_to_all.33 = f32[8,32,256]{2,1,0:T(8,128)S(1)} all-to-all(f32[8,32,256]{2,1,0:T(8,128)S(1)} %bitcast.26), channel_id=1, replica_groups=mesh['yh'=4,'y0'=2,'h'=2,'l'=2,'c'=2,'x'=4,'zl'=2] {'yh','y0'}, dimensions={0} | all-to-all | bytes 524288 | tf_op jit(solution)/shard_map/all_to_all | solution.py:150
  135.6 0.6 reduce_sum.38
  (13 shorter events, 0.2 us)
Async XLA Ops:
  0.0 1.1 copy-start.2
  1.0 0.7 copy-start.1
  35.8 25.0 %collective-permute-start = (f32[8,200,128]{2,1,0:T(8,128)S(1)}, f32[8,200,128]{2,1,0:T(8,128)S(1)}, u32[]{:S(2)}, u32[]{:S(2)}) collective-permute-start(f32[8,200,128]{2,1,0:T(8,128)S(1)} %all_to_all.30.own_ref), channel_id=1, source_target_pairs={{0,8},{8,0},{1,9},{9,1},{2,10},{10,2},{3,11},{11,3},{4,12},{12,4},... | collective-permute-start | bytes 2457608 | tf_op jit(solution)/shard_map/ppermute | solution.py:121
  54.3 1.4 %copy-start = (f32[256,128]{1,0:T(8,128)S(1)}, f32[256,128]{1,0:T(8,128)}, u32[]{:S(2)}) copy-start(f32[256,128]{1,0:T(8,128)} %param.6) | copy-start | bytes 393220
  56.7 19.0 %all-to-all-start.2 = ((f32[4,256,128]{1,2,0:T(8,128)}), f32[4,256,128]{1,2,0:T(8,128)}, u32[]{:S(2)}, u32[]{:S(2)}) async-start(f32[4,256,128]{1,2,0:T(8,128)} %broadcast_in_dim.19), calls=%async_computation.2 | async-start | bytes 1048576 | tf_op jit(solution)/shard_map/all_to_all | solution.py:134
  92.3 14.5 %all-to-all-start.4 = ((f32[8,64,512]{2,1,0:T(8,128)}), f32[8,64,512]{2,1,0:T(8,128)S(1)}, u32[]{:S(2)}, u32[]{:S(2)}) async-start(f32[8,64,512]{2,1,0:T(8,128)} %broadcast_in_dim.20), calls=%async_computation.4 | async-start | bytes 2097152 | tf_op jit(solution)/shard_map/all_to_all | solution.py:142
  108.3 10.0 %collective-permute-start.1 = (f32[256,256]{1,0:T(8,128)S(1)}, f32[256,256]{1,0:T(8,128)S(1)}, u32[]{:S(2)}, u32[]{:S(2)}) collective-permute-start(f32[256,256]{1,0:T(8,128)S(1)} %fusion.1), channel_id=1, source_target_pairs={{0,8},{8,0},{1,9},{9,1},{2,10},{10,2},{3,11},{11,3},{4,12},{12,4},... | collective-permute-start | bytes 786440 | tf_op jit(solution)/shard_map/ppermute | solution.py:149

commit v3 on v2

v3 whole, which is shorter than its diff:
```python
import jax
import jax.numpy as jnp
from jax import lax
from jax.experimental.layout import Layout, with_layout_constraint
from jax.experimental import pallas as pl
from jax.experimental.pallas import tpu as pltpu
from jax.sharding import Mesh, PartitionSpec as P


SOFT2 = 0.05 * 0.05
TINY = 1e-30
GRID = ("yh", "y0", "h", "l", "c")
VEC = ("x", "zl")
SWAP = [(0, 1), (1, 0)]
BF16 = jnp.bfloat16
TAIL = 16
DEPTH = 128


def copies(block, peers):
    return jnp.broadcast_to(block[None], (peers,) + block.shape)


def split(a):
    hi = a.astype(BF16)
    return hi, (a - hi.astype(jnp.float32)).astype(BF16)


def times_transposed(a, b):
    return lax.dot_general(a, b, (((1,), (1,)), ((), ())), preferred_element_type=jnp.float32)


def pieces(a):
    first = a.astype(BF16).astype(jnp.float32)
    second = (a - first).astype(BF16).astype(jnp.float32)
    return first, second, a - first - second


def dist_rows(points, factor, mine):
    p = [factor * x for x in pieces(points)]
    norm = points[0:1] * points[0:1] + points[1:2] * points[1:2] + points[2:3] * points[2:3]
    n = list(pieces(norm))
    one = [jnp.ones_like(norm)] * 3
    if mine:
        rows = [p[0], p[0], p[1], p[1], p[0], p[2]] + n + one
    else:
        rows = [p[0], p[1], p[0], p[1], p[2], p[0]] + one + n
    rows.append(jnp.zeros((DEPTH - 24, points.shape[1]), jnp.float32))
    return jnp.concatenate(rows, axis=0)


def pair_matmul_kernel(origin_ref, own_ref, other_ref, src_ref, out_ref, hi_ref, lo_ref, tgt_ref):
    blocks, _, half = own_ref.shape
    rows = out_ref.shape[1]
    origin = origin_ref[0:3, 0:1]

    @pl.when(pl.program_id(0) == 0)
    def _():
        for j in range(blocks):
            for side, ref in enumerate((own_ref, other_ref)):
                cols = slice(side * half, (side + 1) * half)
                tgt = ref[j, 3 * rows : 3 * rows + 3, :] - origin
                tgt_ref[j, :, cols] = dist_rows(tgt, 1.0, False).astype(BF16)
                moment = None
                for comp in range(3):
                    g = ref[j, comp * rows : (comp + 1) * rows, :]
                    hi, lo = split(g)
                    hi_ref[j, (comp + 1) * rows : (comp + 2) * rows, cols] = hi
                    lo_ref[j, (comp + 1) * rows : (comp + 2) * rows, cols] = lo
                    part = g * tgt[comp : comp + 1]
                    moment = part if moment is None else moment + part
                hi, lo = split(moment)
                hi_ref[j, :rows, cols] = hi
                lo_ref[j, :rows, cols] = lo

    points = src_ref[0, 0:3, :] - origin
    src_rows = dist_rows(points, -2.0, True).T.astype(BF16)
    src_cols = src_ref[0].T
    total = None
    for j in range(blocks):
        dist2 = jnp.dot(src_rows, tgt_ref[j], preferred_element_type=jnp.float32)
        dist2 = jnp.maximum(dist2, TINY)
        grow = 1.0 + dist2 * lax.rsqrt(dist2)
        grow2 = grow * grow
        hi, lo = split(lax.rsqrt((dist2 + SOFT2) * (grow2 * grow2)))
        part = times_transposed(hi, hi_ref[j]) + times_transposed(lo, hi_ref[j]) + times_transposed(hi, lo_ref[j])
        total = part if total is None else total + part
    z = total[:, :rows]
    for comp in range(3):
        away = src_cols[:, comp : comp + 1] - origin_ref[comp : comp + 1, 0:1]
        z = z - away * total[:, (comp + 1) * rows : (comp + 2) * rows]
    out_ref[0] = (0.5 * z).T


def pair_matmul(origin, own, other, src):
    blocks, height, half = own.shape
    rows = (height - TAIL) // 3
    peers, _, per = src.shape
    pairs = peers * per * 2 * half * blocks
    return pl.pallas_call(
        pair_matmul_kernel,
        out_shape=jax.ShapeDtypeStruct((peers, rows, per), jnp.float32),
        grid=(peers,),
        in_specs=[
            pl.BlockSpec((8, half), lambda i: (0, 0)),
            pl.BlockSpec((blocks, height, half), lambda i: (0, 0, 0)),
            pl.BlockSpec((blocks, height, half), lambda i: (0, 0, 0)),
            pl.BlockSpec((1, 8, per), lambda i: (i, 0, 0)),
        ],
        out_specs=pl.BlockSpec((1, rows, per), lambda i: (i, 0, 0)),
        scratch_shapes=[
            pltpu.VMEM((blocks, 4 * rows, 2 * half), BF16),
            pltpu.VMEM((blocks, 4 * rows, 2 * half), BF16),
            pltpu.VMEM((blocks, DEPTH, 2 * half), BF16),
        ],
        compiler_params=pltpu.CompilerParams(
            dimension_semantics=("arbitrary",), vmem_limit_bytes=32 * 1024 * 1024
        ),
        cost_estimate=pl.CostEstimate(
            flops=pairs * (4 * rows * 2 * 3 + 2 * DEPTH),
            bytes_accessed=2 * blocks * height * half * 4 + peers * rows * per * 4,
            transcendentals=2 * pairs,
        ),
    )(origin, own, other, src)


def body(tgt_coords, src_coords, src_values, grad_vectors):
    n = {a: lax.axis_size(a) for a in GRID + VEC}
    nz = n["h"] * n["l"]
    nv = n["x"] * n["zl"]
    slab, pts = src_values.shape
    rows = slab // nz
    piece = rows // n["c"]
    c = lax.axis_index("c")

    own_src = jnp.pad(src_coords, ((0, 5), (0, 0)))
    src_y = lax.all_to_all(copies(own_src, n["yh"]), "yh", 0, 0, tiled=True)
    src_y = src_y[:, :3].reshape(3 * n["yh"], pts)

    grads = grad_vectors.reshape(3, nz, rows, pts).transpose(1, 0, 2, 3).reshape(nz, 3 * rows, pts)
    tail = jnp.concatenate([tgt_coords, src_y, jnp.zeros((1, pts), jnp.float32)], axis=0)
    load = jnp.concatenate([grads, copies(tail, nz)], axis=1)
    load = copies(load, n["y0"]).reshape(n["y0"] * nz, 3 * rows + TAIL, pts)
    own = lax.all_to_all(load, ("y0", "h", "l"), 0, 0, tiled=True)
    src_values, own = lax.optimization_barrier((src_values, own))
    other = lax.ppermute(own, "c", SWAP)

    near = own[:, 3 * rows + 3 : 3 * rows + 3 + 3 * n["yh"], :].reshape(n["y0"], nz, n["yh"], 3, pts)
    near = lax.dynamic_index_in_dim(near, lax.axis_index("y0"), 0, False)
    src = near.transpose(1, 2, 0, 3).reshape(n["yh"], 3, nz * pts)
    src = jnp.pad(src, ((0, 0), (0, 5), (0, 0)))
    origin = jnp.broadcast_to(jnp.mean(src, axis=(0, 2))[:, None], (8, pts))

    rowmajor = Layout(major_to_minor=(0, 1, 2))
    load = with_layout_constraint(copies(src_values, nz), rowmajor)
    values = with_layout_constraint(lax.all_to_all(load, ("h", "l"), 0, 0, tiled=True), rowmajor)

    partial_z = pair_matmul(origin, own, other, src)
    spts = partial_z.shape[2]
    partial_z, values = lax.optimization_barrier((partial_z, values))

    arrived = lax.all_to_all(partial_z, "yh", 0, 0, tiled=True)
    z = arrived.sum(axis=0)
    z_all = lax.all_to_all(copies(z, nv), VEC, 0, 0, tiled=True).reshape(nv, n["c"], piece, spts)
    values = values.transpose(1, 0, 2).reshape(slab, spts)

    def product(core):
        zc = lax.dynamic_index_in_dim(z_all, core, 1, False).reshape(nv * piece, spts)
        return lax.dot_general(zc, values, (((1,), (1,)), ((), ())), precision=lax.Precision.HIGH)

    part = lax.ppermute(product(1 - c), "c", SWAP) + product(c)
    back = lax.all_to_all(part.reshape(nv, piece, slab), ("yh", "y0"), 0, 0, tiled=True)
    return back.sum(axis=0)


def solution(mesh):
    fine = Mesh(mesh.devices.reshape(4, 2, 2, 2, 2, 4, 2), GRID + VEC)

    return jax.shard_map(
        body,
        mesh=fine,
        in_specs=(P(None, GRID), P(None, GRID), P(VEC, GRID), P(None, VEC, GRID)),
        out_specs=P(GRID, VEC),
        check_vma=False,
    )
```

time: 137 us -> 138 us (level)
  blocking collectives: 77.8 us -> 64.9 us
  waiting for transfers between devices: 11.9 us -> 19.5 us
  Pallas kernels: 14.5 us -> 18.9 us
  starting transfers between devices: 21.3 us -> 25.5 us
  matrix products: 2.85 us -> 0.78 us
    all_to_all x1 -> x0, blocking collectives: 12.6 us -> none  [body(): src_all = lax.all_to_all(copies(near, n['yh']), 'yh', 0, 0, tiled=True)]
    all_to_all x1 -> x2, starting transfers between devices: 4.13 us -> 11.1 us  [the longest x1 7.63 us: body(): src_y = lax.all_to_all(copies(own_src, n['yh']), 'yh', 0, 0, tiled=True)]
    all_to_all x1 -> x2, waiting for transfers between devices: 0.31 us -> 5.53 us  [the longest x1 5.53 us: body(): src_y = lax.all_to_all(copies(own_src, n['yh']), 'yh', 0, 0, tiled=True)]
    pallas_call x1, Pallas kernels: 14.5 us -> 18.9 us  [pair_matmul(): pl.pallas_call(pair_matmul_kernel, out_shape=jax.ShapeDtypeStruct((peers,...]
    ppermute x1, starting transfers between devices: 8.84 us -> 5.64 us  [body(): part = lax.ppermute(product(1 - c), 'c', SWAP) + product(c)]
    all_to_all x1, waiting for transfers between devices: 10.5 us -> 12.8 us  [body(): lax.all_to_all(copies(z, nv), VEC, 0, 0, tiled=True)]
    all_to_all x1, blocking collectives: 15.4 us -> 17.5 us  [body(): arrived = lax.all_to_all(partial_z, 'yh', 0, 0, tiled=True)]
    dot_general x2, matrix products: 2.85 us -> 0.78 us  [product(): lax.dot_general(zc, values, (((1,), (1,)), ((), ())), precision=lax.Preci...]
  transfers between devices with their start and end apart: 4 -> 5, of which waited for: 3 -> 3; matrix products, arithmetic and copies ran while one was open for 3% -> 2% of each run, Pallas kernels for 11% -> 14%
where the time goes in v3:
time: 138 us; the launch traced here: 137 us
  blocking collectives  64.9 us (47%)
  starting transfers between devices  25.5 us (18%)
  waiting for transfers between devices  19.5 us (14%)
  Pallas kernels  18.9 us (14%)
  local copies, waits for them, and re-layouts  6.3 us (5%)
    all_to_all x1, blocking collectives, body(): own = lax.all_to_all(load, ('y0', 'h', 'l'), 0, 0, tiled=True)  32.4 us
    pallas_call x1, Pallas kernels, pair_matmul(): pl.pallas_call(pair_matmul_kernel, out_shape=jax.ShapeDtypeStruct((peers,...  18.9 us
    all_to_all x1, blocking collectives, body(): arrived = lax.all_to_all(partial_z, 'yh', 0, 0, tiled=True)  17.5 us
    all_to_all x1, blocking collectives, body(): lax.all_to_all(part.reshape(nv, piece, slab), ('yh', 'y0'), 0, 0, tiled=T...  15 us
    all_to_all x1, waiting for transfers between devices, body(): lax.all_to_all(copies(z, nv), VEC, 0, 0, tiled=True)  12.8 us
    all_to_all x1, starting transfers between devices, body(): src_y = lax.all_to_all(copies(own_src, n['yh']), 'yh', 0, 0, tiled=True)  7.63 us
    ppermute x1, starting transfers between devices, body(): part = lax.ppermute(product(1 - c), 'c', SWAP) + product(c)  5.64 us
    all_to_all x1, waiting for transfers between devices, body(): src_y = lax.all_to_all(copies(own_src, n['yh']), 'yh', 0, 0, tiled=True)  5.53 us
  transfers between devices with their start and end apart: 5, of which 3 were waited for; matrix products, arithmetic and copies ran while one was open for 2% of the time, Pallas kernels for 14%

profile of v3, /device:TPU:1, one launch (start us, length us, event | category | flops | bytes accessed | tf_op | source)
XLA Modules:
  0.0 137.0 jit_solution(16640706724634485795)
XLA Ops:
  0.0 0.7 pad.8
  0.7 0.6 broadcast_in_dim.14
  1.3 7.6 %all-to-all-start = ((f32[4,8,128]{2,1,0:T(8,128)}), f32[4,8,128]{2,1,0:T(8,128)S(1)}, u32[]{:S(2)}, u32[]{:S(2)}) async-start(f32[4,8,128]{2,1,0:T(8,128)} %broadcast_in_dim.14), calls=%async_computation | async-start | bytes 32768 | tf_op jit(solution)/shard_map/all_to_all | solution.py:137
  8.9 1.0 copy.9
  10.0 0.1 pad.14.clone
  10.0 5.5 %all-to-all-done = f32[4,8,128]{2,1,0:T(8,128)S(1)} async-done(((f32[4,8,128]{2,1,0:T(8,128)}), f32[4,8,128]{2,1,0:T(8,128)S(1)}, u32[]{:S(2)}, u32[]{:S(2)}) %all-to-all-start) | async-done | bytes 16416 | tf_op jit(solution)/shard_map/all_to_all | solution.py:137
  15.6 0.0 copy-start.1
  15.6 0.7 copy-done.1
  16.2 0.1 maximum_maximum_fusion
  16.4 0.1 broadcast_in_dim.17
  16.4 32.4 %all_to_all.30.own_ref = f32[8,208,128]{2,1,0:T(8,128)S(1)} all-to-all(f32[8,208,128]{2,1,0:T(8,128)S(1)} %bitcast.24), channel_id=1, replica_groups=mesh['yh'=4,'y0'=2,'h'=2,'l'=2,'c'=2,'x'=4,'zl'=2] {'y0','h','l'}, dimensions={0} | all-to-all | bytes 1703936 | tf_op jit(solution)/shard_map/all_to_all | solution.py:144
  48.8 4.8 %collective-permute-start = (f32[8,208,128]{2,1,0:T(8,128)S(1)}, f32[8,208,128]{2,1,0:T(8,128)S(1)}, u32[]{:S(2)}, u32[]{:S(2)}) collective-permute-start(f32[8,208,128]{2,1,0:T(8,128)S(1)} %all_to_all.30.own_ref), channel_id=1, source_target_pairs={{0,8},{8,0},{1,9},{9,1},{2,10},{10,2},{3,11},{11,3},{4,12},{12,4},... | collective-permute-start | bytes 2555912 | tf_op jit(solution)/shard_map/ppermute | solution.py:146
  53.7 0.0 copy-start
  53.8 0.8 copy-done
  54.6 0.8 broadcast_in_dim.19
  55.4 3.5 %all-to-all-start.2 = ((f32[4,256,128]{2,1,0:T(8,128)}), f32[4,256,128]{2,1,0:T(8,128)S(1)}, u32[]{:S(2)}, u32[]{:S(2)}) async-start(f32[4,256,128]{2,1,0:T(8,128)} %broadcast_in_dim.19), calls=%async_computation.2 | async-start | bytes 1048576 | tf_op jit(solution)/shard_map/all_to_all | solution.py:156
  58.9 0.1 fusion
  59.0 0.0 collective-permute-done.other_ref
  59.0 0.1 broadcast_in_dim.18.origin_ref
  59.1 18.9 %shard_map.46 = f32[4,64,512]{2,1,0:T(8,128)S(1)} custom-call(f32[8,128]{1,0:T(8,128)S(1)} %broadcast_in_dim.18.origin_ref, f32[8,208,128]{2,1,0:T(8,128)S(1)} %all_to_all.30.own_ref, f32[8,208,128]{2,1,0:T(8,128)S(1)} %collective-permute-done.other_ref, f32[4,8,512]{2,1,0:T(8,128)S(1)} %get-tuple-element.15.src_ref), custom_call_target="tpu_custom_call" | custom-call | flops 7516192768 | bytes 2228224 | tf_op jit(solution)/shard_map/pallas_call | solution.py:100
  78.0 0.0 all-to-all-done.2
  78.0 17.5 %all_to_all.31 = f32[4,64,512]{2,1,0:T(8,128)S(1)} all-to-all(f32[4,64,512]{2,1,0:T(8,128)S(1)} %shard_map.46), channel_id=1, replica_groups=mesh['yh'=4,'y0'=2,'h'=2,'l'=2,'c'=2,'x'=4,'zl'=2] {'yh'}, dimensions={0} | all-to-all | bytes 1048576 | tf_op jit(solution)/shard_map/all_to_all | solution.py:162
  95.6 1.1 broadcast_in_dim.20
  96.7 4.0 %all-to-all-start.4 = ((f32[8,64,512]{2,1,0:T(8,128)}), f32[8,64,512]{2,1,0:T(8,128)S(1)}, u32[]{:S(2)}, u32[]{:S(2)}) async-start(f32[8,64,512]{2,1,0:T(8,128)} %broadcast_in_dim.20), calls=%async_computation.4 | async-start | bytes 2097152 | tf_op jit(solution)/shard_map/all_to_all | solution.py:164
  100.7 0.2 copy.14
  100.9 12.8 %all-to-all-done.4 = f32[8,64,512]{2,1,0:T(8,128)S(1)} async-done(((f32[8,64,512]{2,1,0:T(8,128)}), f32[8,64,512]{2,1,0:T(8,128)S(1)}, u32[]{:S(2)}, u32[]{:S(2)}) %all-to-all-start.4) | async-done | bytes 1048608 | tf_op jit(solution)/shard_map/all_to_all | solution.py:164
  113.7 0.1 constant_dynamic-slice_fusion
  113.8 0.4 fusion.1
  114.2 5.6 %collective-permute-start.1 = (f32[256,256]{1,0:T(8,128)S(1)}, f32[256,256]{1,0:T(8,128)S(1)}, u32[]{:S(2)}, u32[]{:S(2)}) collective-permute-start(f32[256,256]{1,0:T(8,128)S(1)} %fusion.1), channel_id=1, source_target_pairs={{0,8},{8,0},{1,9},{9,1},{2,10},{10,2},{3,11},{11,3},{4,12},{12,4},... | collective-permute-start | bytes 786440 | tf_op jit(solution)/shard_map/ppermute | solution.py:171
  119.8 1.1 collective-permute-done.1
  121.0 0.4 convolution_add_fusion
  121.4 15.0 %all_to_all.32 = f32[8,32,256]{2,1,0:T(8,128)S(1)} all-to-all(f32[8,32,256]{2,1,0:T(8,128)S(1)} %bitcast.29), channel_id=1, replica_groups=mesh['yh'=4,'y0'=2,'h'=2,'l'=2,'c'=2,'x'=4,'zl'=2] {'yh','y0'}, dimensions={0} | all-to-all | bytes 524288 | tf_op jit(solution)/shard_map/all_to_all | solution.py:172
  136.3 0.6 reduce_sum.29
  (10 shorter events, 0.2 us)
Async XLA Ops:
  1.3 14.3 %all-to-all-start = ((f32[4,8,128]{2,1,0:T(8,128)}), f32[4,8,128]{2,1,0:T(8,128)S(1)}, u32[]{:S(2)}, u32[]{:S(2)}) async-start(f32[4,8,128]{2,1,0:T(8,128)} %broadcast_in_dim.14), calls=%async_computation | async-start | bytes 32768 | tf_op jit(solution)/shard_map/all_to_all | solution.py:137
  15.6 0.7 copy-start.1
  48.8 10.2 %collective-permute-start = (f32[8,208,128]{2,1,0:T(8,128)S(1)}, f32[8,208,128]{2,1,0:T(8,128)S(1)}, u32[]{:S(2)}, u32[]{:S(2)}) collective-permute-start(f32[8,208,128]{2,1,0:T(8,128)S(1)} %all_to_all.30.own_ref), channel_id=1, source_target_pairs={{0,8},{8,0},{1,9},{9,1},{2,10},{10,2},{3,11},{11,3},{4,12},{12,4},... | collective-permute-start | bytes 2555912 | tf_op jit(solution)/shard_map/ppermute | solution.py:146
  53.7 0.9 copy-start
  55.4 22.6 %all-to-all-start.2 = ((f32[4,256,128]{2,1,0:T(8,128)}), f32[4,256,128]{2,1,0:T(8,128)S(1)}, u32[]{:S(2)}, u32[]{:S(2)}) async-start(f32[4,256,128]{2,1,0:T(8,128)} %broadcast_in_dim.19), calls=%async_computation.2 | async-start | bytes 1048576 | tf_op jit(solution)/shard_map/all_to_all | solution.py:156
  96.7 17.0 %all-to-all-start.4 = ((f32[8,64,512]{2,1,0:T(8,128)}), f32[8,64,512]{2,1,0:T(8,128)S(1)}, u32[]{:S(2)}, u32[]{:S(2)}) async-start(f32[8,64,512]{2,1,0:T(8,128)} %broadcast_in_dim.20), calls=%async_computation.4 | async-start | bytes 2097152 | tf_op jit(solution)/shard_map/all_to_all | solution.py:164
  114.2 6.8 %collective-permute-start.1 = (f32[256,256]{1,0:T(8,128)S(1)}, f32[256,256]{1,0:T(8,128)S(1)}, u32[]{:S(2)}, u32[]{:S(2)}) collective-permute-start(f32[256,256]{1,0:T(8,128)S(1)} %fusion.1), channel_id=1, source_target_pairs={{0,8},{8,0},{1,9},{9,1},{2,10},{10,2},{3,11},{11,3},{4,12},{12,4},... | collective-permute-start | bytes 786440 | tf_op jit(solution)/shard_map/ppermute | solution.py:171

commit v4 on v2

--- a/solution.py
+++ b/solution.py
@@ -12,7 +12,7 @@
 VEC = ("x", "zl")
 SWAP = [(0, 1), (1, 0)]
 BF16 = jnp.bfloat16
-TAIL = 8
+TAIL = 16
 
 
 def copies(block, peers):
@@ -28,7 +28,8 @@
     return lax.dot_general(a, b, (((1,), (1,)), ((), ())), preferred_element_type=jnp.float32)
 
 
-def pair_matmul_kernel(origin_ref, own_ref, other_ref, src_ref, out_ref, hi_ref, lo_ref):
+def pair_matmul_kernel(*refs):
+    origin_ref, own_ref, other_ref, src_ref, *earlier, out_ref, hi_ref, lo_ref = refs
     blocks, _, half = own_ref.shape
     rows = out_ref.shape[1]
     origin = [origin_ref[comp : comp + 1, 0:1] for comp in range(3)]
@@ -50,7 +51,8 @@
                 hi_ref[j, :rows, cols] = hi
                 lo_ref[j, :rows, cols] = lo
 
-    src = [src_ref[:, comp : comp + 1] for comp in range(3)]
+    src_cols = src_ref[0].T
+    src = [src_cols[:, comp : comp + 1] for comp in range(3)]
     total = None
     for j in range(blocks):
         dist2 = None
@@ -67,29 +69,33 @@
     z = total[:, :rows]
     for comp in range(3):
         z = z - (src[comp] - origin[comp]) * total[:, (comp + 1) * rows : (comp + 2) * rows]
-    out_ref[0] = (0.5 * z).T
+    z = (0.5 * z).T
+    for ref in earlier:
+        z = z + ref[0]
+    out_ref[0] = z
 
 
-def pair_matmul(origin, own, other, src_cols, peers):
+def pair_matmul(origin, own, other, src, *earlier):
     blocks, height, half = own.shape
     rows = (height - TAIL) // 3
-    total_s = src_cols.shape[0]
-    per = total_s // peers
-    step = STEP
-    inner = per // step
-    pairs = total_s * 2 * half * blocks
+    peers, _, per = src.shape
+    pairs = peers * per * 2 * half * blocks
     return pl.pallas_call(
         pair_matmul_kernel,
         out_shape=jax.ShapeDtypeStruct((peers, rows, per), jnp.float32),
-        grid=(total_s // step,),
+        grid=(peers,),
         in_specs=[
             pl.BlockSpec((8, half), lambda i: (0, 0)),
             pl.BlockSpec((blocks, height, half), lambda i: (0, 0, 0)),
             pl.BlockSpec((blocks, height, half), lambda i: (0, 0, 0)),
-            pl.BlockSpec((step, 8), lambda i: (i, 0)),
+            pl.BlockSpec((1, 8, per), lambda i: (i, 0, 0)),
+        ]
+        + [pl.BlockSpec((1, rows, per), lambda i: (i, 0, 0))] * len(earlier),
+        out_specs=pl.BlockSpec((1, rows, per), lambda i: (i, 0, 0)),
+        scratch_shapes=[
+            pltpu.VMEM((blocks, 4 * rows, 2 * half), BF16),
+            pltpu.VMEM((blocks, 4 * rows, 2 * half), BF16),
         ],
-        out_specs=pl.BlockSpec((1, rows, step), lambda i: (i // inner, 0, i % inner)),
-        scratch_shapes=[pltpu.VMEM((blocks, 4 * rows, 2 * half), BF16)] * 2,
         compiler_params=pltpu.CompilerParams(
             dimension_semantics=("arbitrary",), vmem_limit_bytes=32 * 1024 * 1024
         ),
@@ -98,10 +104,7 @@
             bytes_accessed=2 * blocks * height * half * 4 + peers * rows * per * 4,
             transcendentals=2 * pairs,
         ),
-    )(origin, own, other, src_cols)
-
-
-STEP = 512
+    )(origin, own, other, src, *earlier)
 
 
 def body(tgt_coords, src_coords, src_values, grad_vectors):
@@ -113,34 +116,37 @@
     piece = rows // n["c"]
     c = lax.axis_index("c")
 
+    own_src = jnp.pad(src_coords, ((0, 5), (0, 0)))
+    src_y = lax.all_to_all(copies(own_src, n["yh"]), "yh", 0, 0, tiled=True)
+    src_y = src_y[:, :3].reshape(3 * n["yh"], pts)
+
     grads = grad_vectors.reshape(3, nz, rows, pts).transpose(1, 0, 2, 3).reshape(nz, 3 * rows, pts)
-    tail = jnp.concatenate([tgt_coords, src_coords, jnp.zeros((TAIL - 6, pts), jnp.float32)], axis=0)
+    tail = jnp.concatenate([tgt_coords, src_y, jnp.zeros((1, pts), jnp.float32)], axis=0)
     load = jnp.concatenate([grads, copies(tail, nz)], axis=1)
-    load = copies(load, n["y0"]).reshape(n["y0"] * nz, 3 * rows + TAIL, pts)
-    own = lax.all_to_all(load, ("y0", "h", "l"), 0, 0, tiled=True)
-    other = lax.ppermute(own, "c", SWAP)
+    own = lax.all_to_all(load, ("h", "l"), 0, 0, tiled=True)
+    far = lax.ppermute(own, "y0", SWAP)
+    own_other = lax.ppermute(own, "c", SWAP)
 
-    near = own[:, 3 * rows + 3 : 3 * rows + 6, :].reshape(n["y0"], 3 * nz, pts)
-    near = lax.dynamic_index_in_dim(near, lax.axis_index("y0"), 0, False)
-    near = jnp.pad(near, ((0, 4), (0, 0)))
-    src_all = lax.all_to_all(copies(near, n["yh"]), "yh", 0, 0, tiled=True)
-    src_all = src_all[:, : 3 * nz].reshape(n["yh"] * nz, 3, pts)
-    src_cols = src_all.transpose(0, 2, 1).reshape(n["yh"] * nz * pts, 3)
-    src_cols = jnp.pad(src_cols, ((0, 0), (0, 5)))
-    origin = jnp.mean(src_all, axis=(0, 2))
-    origin = jnp.broadcast_to(jnp.pad(origin, (0, 5))[:, None], (8, pts))
-    src_values, src_cols = lax.optimization_barrier((src_values, src_cols))
+    near = own[:, 3 * rows + 3 : 3 * rows + 3 + 3 * n["yh"], :].reshape(nz, n["yh"], 3, pts)
+    src = near.transpose(1, 2, 0, 3).reshape(n["yh"], 3, nz * pts)
+    src = jnp.pad(src, ((0, 0), (0, 5), (0, 0)))
+    origin = jnp.broadcast_to(jnp.mean(src, axis=(0, 2))[:, None], (8, pts))
 
-    values = lax.all_to_all(copies(src_values, nz), ("h", "l"), 0, 0, tiled=True)
-
-    partial_z = pair_matmul(origin, own, other, src_cols, n["yh"])
+    partial_z = pair_matmul(origin, own, own_other, src)
+    far_other = lax.ppermute(far, "c", SWAP)
+    partial_z = pair_matmul(origin, far, far_other, src, partial_z)
     spts = partial_z.shape[2]
-    partial_z, values = lax.optimization_barrier((partial_z, values))
+    src_values, partial_z = lax.optimization_barrier((src_values, partial_z))
 
     arrived = lax.all_to_all(partial_z, "yh", 0, 0, tiled=True)
+    v_l = lax.ppermute(src_values, "l", SWAP)
+    v_h = lax.ppermute(src_values, "h", SWAP)
+    v_hl = lax.ppermute(src_values, ("h", "l"), [(i, 3 - i) for i in range(4)])
+    me = lax.axis_index(("h", "l"))
+    stack = jnp.stack([src_values, v_l, v_h, v_hl])
+    values = jnp.concatenate([lax.dynamic_index_in_dim(stack, me ^ b, 0, False) for b in range(4)], axis=1)
     z = arrived.sum(axis=0)
     z_all = lax.all_to_all(copies(z, nv), VEC, 0, 0, tiled=True).reshape(nv, n["c"], piece, spts)
-    values = values.transpose(1, 0, 2).reshape(slab, spts)
 
     def product(core):
         zc = lax.dynamic_index_in_dim(z_all, core, 1, False).reshape(nv * piece, spts)

time: 137 us -> 144 us (1.051)
  the two profiles are of different devices: /device:TPU:1 before, /device:TPU:66 now
where the time goes in v4:
time: 144 us; the launch traced here: 143 us
  blocking collectives  56.5 us (39%)
  starting transfers between devices  33.5 us (23%)
  waiting for transfers between devices  28.2 us (20%)
  Pallas kernels  18.6 us (13%)
  local copies, waits for them, and re-layouts  4.44 us (3%)
    all_to_all x1, blocking collectives, body(): own = lax.all_to_all(load, ('h', 'l'), 0, 0, tiled=True)  21.4 us
    all_to_all x1, blocking collectives, body(): arrived = lax.all_to_all(partial_z, 'yh', 0, 0, tiled=True)  19.6 us
    pallas_call x2, Pallas kernels, pair_matmul(): pl.pallas_call(pair_matmul_kernel, out_shape=jax.ShapeDtypeStruct((peers,...  18.6 us
    all_to_all x1, blocking collectives, body(): lax.all_to_all(part.reshape(nv, piece, slab), ('yh', 'y0'), 0, 0, tiled=T...  15.5 us
    ppermute x1, waiting for transfers between devices, body(): far = lax.ppermute(own, 'y0', SWAP)  8.4 us
    ppermute x1, waiting for transfers between devices, body(): v_hl = lax.ppermute(src_values, ('h', 'l'), [(i, 3 - i) for i in range(4)])  8.16 us
    all_to_all x1, starting transfers between devices, body(): src_y = lax.all_to_all(copies(own_src, n['yh']), 'yh', 0, 0, tiled=True)  7.09 us
    all_to_all x1, waiting for transfers between devices, body(): src_y = lax.all_to_all(copies(own_src, n['yh']), 'yh', 0, 0, tiled=True)  6.68 us
  transfers between devices with their start and end apart: 9, of which 5 were waited for; matrix products, arithmetic and copies ran while one was open for 1% of the time, Pallas kernels for 6%

profile of v4, /device:TPU:66, one launch (start us, length us, event | category | flops | bytes accessed | tf_op | source)
XLA Modules:
  0.0 143.3 jit_solution(13266048502866344462)
XLA Ops:
  0.0 0.7 pad.8
  0.7 0.6 broadcast_in_dim.10
  1.3 7.1 %all-to-all-start = ((f32[4,8,128]{2,1,0:T(8,128)}), f32[4,8,128]{2,1,0:T(8,128)S(1)}, u32[]{:S(2)}, u32[]{:S(2)}) async-start(f32[4,8,128]{2,1,0:T(8,128)} %broadcast_in_dim.10), calls=%async_computation | async-start | bytes 32768 | tf_op jit(solution)/shard_map/all_to_all | solution.py:120
  8.4 1.0 copy.7
  9.4 0.1 pad.22.clone
  9.5 6.7 %all-to-all-done = f32[4,8,128]{2,1,0:T(8,128)S(1)} async-done(((f32[4,8,128]{2,1,0:T(8,128)}), f32[4,8,128]{2,1,0:T(8,128)S(1)}, u32[]{:S(2)}, u32[]{:S(2)}) %all-to-all-start) | async-done | bytes 16416 | tf_op jit(solution)/shard_map/all_to_all | solution.py:120
  16.2 0.0 copy-start.1
  16.2 0.7 copy-done.1
  16.9 0.1 maximum_maximum_fusion
  17.0 21.4 %all_to_all.25.refs_1_ = f32[4,208,128]{2,1,0:T(8,128)S(1)} all-to-all(f32[4,208,128]{2,1,0:T(8,128)S(1)} %pad_maximum_fusion.2), channel_id=1, replica_groups=mesh['yh'=4,'y0'=2,'h'=2,'l'=2,'c'=2,'x'=4,'zl'=2] {'h','l'}, dimensions={0} | all-to-all | bytes 851968 | tf_op jit(solution)/shard_map/all_to_all | solution.py:126
  38.4 2.6 %collective-permute-start = (f32[4,208,128]{2,1,0:T(8,128)S(1)}, f32[4,208,128]{2,1,0:T(8,128)S(1)}, u32[]{:S(2)}, u32[]{:S(2)}) collective-permute-start(f32[4,208,128]{2,1,0:T(8,128)S(1)} %all_to_all.25.refs_1_), channel_id=1, source_target_pairs={{0,64},{64,0},{1,65},{65,1},{2,66},{66,2},{3,67},{67,3},{4,68},{68... | collective-permute-start | bytes 1277960 | tf_op jit(solution)/shard_map/ppermute | solution.py:127
  41.0 1.9 %collective-permute-start.2 = (f32[4,208,128]{2,1,0:T(8,128)S(1)}, f32[4,208,128]{2,1,0:T(8,128)S(1)}, u32[]{:S(2)}, u32[]{:S(2)}) collective-permute-start(f32[4,208,128]{2,1,0:T(8,128)S(1)} %all_to_all.25.refs_1_), channel_id=1, source_target_pairs={{0,8},{8,0},{1,9},{9,1},{2,10},{10,2},{3,11},{11,3},{4,12},{12,4},... | collective-permute-start | bytes 1277960 | tf_op jit(solution)/shard_map/ppermute | solution.py:128
  42.9 0.1 fusion.3
  43.1 8.4 %collective-permute-done.refs_1_ = f32[4,208,128]{2,1,0:T(8,128)S(1)} collective-permute-done((f32[4,208,128]{2,1,0:T(8,128)S(1)}, f32[4,208,128]{2,1,0:T(8,128)S(1)}, u32[]{:S(2)}, u32[]{:S(2)}) %collective-permute-start) | collective-permute-done | bytes 426016 | tf_op jit(solution)/shard_map/ppermute | solution.py:127
  51.5 1.9 %collective-permute-start.1 = (f32[4,208,128]{2,1,0:T(8,128)S(1)}, f32[4,208,128]{2,1,0:T(8,128)S(1)}, u32[]{:S(2)}, u32[]{:S(2)}) collective-permute-start(f32[4,208,128]{2,1,0:T(8,128)S(1)} %collective-permute-done.refs_1_), channel_id=1, source_target_pairs={{0,8},{8,0},{1,9},{9,1},{2,10},{10,2},{3,11},{11,3},{4,12},{12,4},... | collective-permute-start | bytes 1277960 | tf_op jit(solution)/shard_map/ppermute | solution.py:136
  53.4 0.0 collective-permute-done.2.refs_2_
  53.4 0.1 broadcast_in_dim.13.refs_0_
  53.5 9.3 %shard_map.46.refs_4_ = f32[4,64,512]{2,1,0:T(8,128)S(1)} custom-call(f32[8,128]{1,0:T(8,128)S(1)} %broadcast_in_dim.13.refs_0_, f32[4,208,128]{2,1,0:T(8,128)S(1)} %all_to_all.25.refs_1_, f32[4,208,128]{2,1,0:T(8,128)S(1)} %collective-permute-done.2.refs_2_, f32[4,8,512]{2,1,0:T(8,128)S(1)} %get-tuple-element.15.refs_3_), custom_call_target="tpu_custom_call" | custom-call | flops 3221225472 | bytes 1376256 | tf_op jit(solution)/shard_map/pallas_call | solution.py:83
  62.8 0.0 collective-permute-done.1.refs_2_
  62.8 9.3 %shard_map.47 = f32[4,64,512]{2,1,0:T(8,128)S(1)} custom-call(f32[8,128]{1,0:T(8,128)S(1)} %broadcast_in_dim.13.refs_0_, f32[4,208,128]{2,1,0:T(8,128)S(1)} %collective-permute-done.refs_1_, f32[4,208,128]{2,1,0:T(8,128)S(1)} %collective-permute-done.1.refs_2_, f32[4,8,512]{2,1,0:T(8,128)S(1)} %get-tuple-element.15.refs_3_, f32[4,64,512]{2,1,0:T(8,128)S(1)} %shard_map.46.refs_4_), custom_call_target="tpu_custom_call" | custom-call | flops 3221225472 | bytes 1376256 | tf_op jit(solution)/shard_map/pallas_call | solution.py:83
  72.1 19.6 %all_to_all.26 = f32[4,64,512]{2,1,0:T(8,128)S(1)} all-to-all(f32[4,64,512]{2,1,0:T(8,128)S(1)} %shard_map.47), channel_id=1, replica_groups=mesh['yh'=4,'y0'=2,'h'=2,'l'=2,'c'=2,'x'=4,'zl'=2] {'yh'}, dimensions={0} | all-to-all | bytes 1048576 | tf_op jit(solution)/shard_map/all_to_all | solution.py:141
  91.8 1.1 broadcast_in_dim.14
  92.9 0.0 copy-start
  92.9 5.9 %all-to-all-start.3 = ((f32[8,64,512]{2,1,0:T(8,128)}), f32[8,64,512]{2,1,0:T(8,128)S(1)}, u32[]{:S(2)}, u32[]{:S(2)}) async-start(f32[8,64,512]{2,1,0:T(8,128)} %broadcast_in_dim.14), calls=%async_computation.3 | async-start | bytes 2097152 | tf_op jit(solution)/shard_map/all_to_all | solution.py:149
  98.8 0.0 copy-done
  98.8 3.5 %collective-permute-start.5 = (f32[256,128]{1,0:T(8,128)S(1)}, f32[256,128]{1,0:T(8,128)S(1)}, u32[]{:S(2)}, u32[]{:S(2)}) collective-permute-start(f32[256,128]{1,0:T(8,128)S(1)} %copy-done), channel_id=1, source_target_pairs={{0,48},{16,32},{32,16},{48,0},{1,49},{17,33},{33,17},{49,1},{2,50}... | collective-permute-start | bytes 393224 | tf_op jit(solution)/shard_map/ppermute | solution.py:144
  102.3 3.5 %collective-permute-start.4 = (f32[256,128]{1,0:T(8,128)S(1)}, f32[256,128]{1,0:T(8,128)S(1)}, u32[]{:S(2)}, u32[]{:S(2)}) collective-permute-start(f32[256,128]{1,0:T(8,128)S(1)} %copy-done), channel_id=1, source_target_pairs={{0,32},{32,0},{1,33},{33,1},{2,34},{34,2},{3,35},{35,3},{4,36},{36... | collective-permute-start | bytes 393224 | tf_op jit(solution)/shard_map/ppermute | solution.py:143
  105.8 5.2 %collective-permute-start.3 = (f32[256,128]{1,0:T(8,128)S(1)}, f32[256,128]{1,0:T(8,128)S(1)}, u32[]{:S(2)}, u32[]{:S(2)}) collective-permute-start(f32[256,128]{1,0:T(8,128)S(1)} %copy-done), channel_id=1, source_target_pairs={{0,16},{16,0},{1,17},{17,1},{2,18},{18,2},{3,19},{19,3},{4,20},{20... | collective-permute-start | bytes 393224 | tf_op jit(solution)/shard_map/ppermute | solution.py:142
  111.0 8.2 %collective-permute-done.5 = f32[256,128]{1,0:T(8,128)S(1)} collective-permute-done((f32[256,128]{1,0:T(8,128)S(1)}, f32[256,128]{1,0:T(8,128)S(1)}, u32[]{:S(2)}, u32[]{:S(2)}) %collective-permute-start.5) | collective-permute-done | bytes 131104 | tf_op jit(solution)/shard_map/ppermute | solution.py:144
  119.2 3.5 %collective-permute-done.4 = f32[256,128]{1,0:T(8,128)S(1)} collective-permute-done((f32[256,128]{1,0:T(8,128)S(1)}, f32[256,128]{1,0:T(8,128)S(1)}, u32[]{:S(2)}, u32[]{:S(2)}) %collective-permute-start.4) | collective-permute-done | bytes 131104 | tf_op jit(solution)/shard_map/ppermute | solution.py:143
  122.7 0.0 collective-permute-done.3
  122.8 0.0 all-to-all-done.3
  122.8 0.1 constant_dynamic-slice_fusion
  122.9 0.4 fusion
  123.3 1.9 %collective-permute-start.6 = (f32[256,256]{1,0:T(8,128)S(1)}, f32[256,256]{1,0:T(8,128)S(1)}, u32[]{:S(2)}, u32[]{:S(2)}) collective-permute-start(f32[256,256]{1,0:T(8,128)S(1)} %fusion), channel_id=1, source_target_pairs={{0,8},{8,0},{1,9},{9,1},{2,10},{10,2},{3,11},{11,3},{4,12},{12,4},... | collective-permute-start | bytes 786440 | tf_op jit(solution)/shard_map/ppermute | solution.py:155
  125.3 1.5 %collective-permute-done.6 = f32[256,256]{1,0:T(8,128)S(1)} collective-permute-done((f32[256,256]{1,0:T(8,128)S(1)}, f32[256,256]{1,0:T(8,128)S(1)}, u32[]{:S(2)}, u32[]{:S(2)}) %collective-permute-start.6) | collective-permute-done | bytes 262176 | tf_op jit(solution)/shard_map/ppermute | solution.py:155
  126.8 0.4 convolution_add_fusion
  127.2 15.5 %all_to_all.27 = f32[8,32,256]{2,1,0:T(8,128)S(1)} all-to-all(f32[8,32,256]{2,1,0:T(8,128)S(1)} %bitcast.30), channel_id=1, replica_groups=mesh['yh'=4,'y0'=2,'h'=2,'l'=2,'c'=2,'x'=4,'zl'=2] {'yh','y0'}, dimensions={0} | all-to-all | bytes 524288 | tf_op jit(solution)/shard_map/all_to_all | solution.py:156
  142.6 0.6 reduce_sum.29
  (11 shorter events, 0.2 us)
Async XLA Ops:
  1.3 14.9 %all-to-all-start = ((f32[4,8,128]{2,1,0:T(8,128)}), f32[4,8,128]{2,1,0:T(8,128)S(1)}, u32[]{:S(2)}, u32[]{:S(2)}) async-start(f32[4,8,128]{2,1,0:T(8,128)} %broadcast_in_dim.10), calls=%async_computation | async-start | bytes 32768 | tf_op jit(solution)/shard_map/all_to_all | solution.py:120
  16.2 0.7 copy-start.1
  38.4 13.1 %collective-permute-start = (f32[4,208,128]{2,1,0:T(8,128)S(1)}, f32[4,208,128]{2,1,0:T(8,128)S(1)}, u32[]{:S(2)}, u32[]{:S(2)}) collective-permute-start(f32[4,208,128]{2,1,0:T(8,128)S(1)} %all_to_all.25.refs_1_), channel_id=1, source_target_pairs={{0,64},{64,0},{1,65},{65,1},{2,66},{66,2},{3,67},{67,3},{4,68},{68... | collective-permute-start | bytes 1277960 | tf_op jit(solution)/shard_map/ppermute | solution.py:127
  41.0 12.4 %collective-permute-start.2 = (f32[4,208,128]{2,1,0:T(8,128)S(1)}, f32[4,208,128]{2,1,0:T(8,128)S(1)}, u32[]{:S(2)}, u32[]{:S(2)}) collective-permute-start(f32[4,208,128]{2,1,0:T(8,128)S(1)} %all_to_all.25.refs_1_), channel_id=1, source_target_pairs={{0,8},{8,0},{1,9},{9,1},{2,10},{10,2},{3,11},{11,3},{4,12},{12,4},... | collective-permute-start | bytes 1277960 | tf_op jit(solution)/shard_map/ppermute | solution.py:128
  51.5 11.3 %collective-permute-start.1 = (f32[4,208,128]{2,1,0:T(8,128)S(1)}, f32[4,208,128]{2,1,0:T(8,128)S(1)}, u32[]{:S(2)}, u32[]{:S(2)}) collective-permute-start(f32[4,208,128]{2,1,0:T(8,128)S(1)} %collective-permute-done.refs_1_), channel_id=1, source_target_pairs={{0,8},{8,0},{1,9},{9,1},{2,10},{10,2},{3,11},{11,3},{4,12},{12,4},... | collective-permute-start | bytes 1277960 | tf_op jit(solution)/shard_map/ppermute | solution.py:136
  92.9 5.9 %copy-start = (f32[256,128]{1,0:T(8,128)S(1)}, f32[256,128]{1,0:T(8,128)}, u32[]{:S(2)}) copy-start(f32[256,128]{1,0:T(8,128)} %param.6) | copy-start | bytes 393220
  92.9 29.9 %all-to-all-start.3 = ((f32[8,64,512]{2,1,0:T(8,128)}), f32[8,64,512]{2,1,0:T(8,128)S(1)}, u32[]{:S(2)}, u32[]{:S(2)}) async-start(f32[8,64,512]{2,1,0:T(8,128)} %broadcast_in_dim.14), calls=%async_computation.3 | async-start | bytes 2097152 | tf_op jit(solution)/shard_map/all_to_all | solution.py:149
  98.8 20.4 %collective-permute-start.5 = (f32[256,128]{1,0:T(8,128)S(1)}, f32[256,128]{1,0:T(8,128)S(1)}, u32[]{:S(2)}, u32[]{:S(2)}) collective-permute-start(f32[256,128]{1,0:T(8,128)S(1)} %copy-done), channel_id=1, source_target_pairs={{0,48},{16,32},{32,16},{48,0},{1,49},{17,33},{33,17},{49,1},{2,50}... | collective-permute-start | bytes 393224 | tf_op jit(solution)/shard_map/ppermute | solution.py:144
  102.3 20.4 %collective-permute-start.4 = (f32[256,128]{1,0:T(8,128)S(1)}, f32[256,128]{1,0:T(8,128)S(1)}, u32[]{:S(2)}, u32[]{:S(2)}) collective-permute-start(f32[256,128]{1,0:T(8,128)S(1)} %copy-done), channel_id=1, source_target_pairs={{0,32},{32,0},{1,33},{33,1},{2,34},{34,2},{3,35},{35,3},{4,36},{36... | collective-permute-start | bytes 393224 | tf_op jit(solution)/shard_map/ppermute | solution.py:143
  105.8 16.9 %collective-permute-start.3 = (f32[256,128]{1,0:T(8,128)S(1)}, f32[256,128]{1,0:T(8,128)S(1)}, u32[]{:S(2)}, u32[]{:S(2)}) collective-permute-start(f32[256,128]{1,0:T(8,128)S(1)} %copy-done), channel_id=1, source_target_pairs={{0,16},{16,0},{1,17},{17,1},{2,18},{18,2},{3,19},{19,3},{4,20},{20... | collective-permute-start | bytes 393224 | tf_op jit(solution)/shard_map/ppermute | solution.py:142
  123.3 3.4 %collective-permute-start.6 = (f32[256,256]{1,0:T(8,128)S(1)}, f32[256,256]{1,0:T(8,128)S(1)}, u32[]{:S(2)}, u32[]{:S(2)}) collective-permute-start(f32[256,256]{1,0:T(8,128)S(1)} %fusion), channel_id=1, source_target_pairs={{0,8},{8,0},{1,9},{9,1},{2,10},{10,2},{3,11},{11,3},{4,12},{12,4},... | collective-permute-start | bytes 786440 | tf_op jit(solution)/shard_map/ppermute | solution.py:155

commit v5 on v2

--- a/solution.py
+++ b/solution.py
@@ -1,6 +1,7 @@
 import jax
 import jax.numpy as jnp
 from jax import lax
+from jax.experimental.layout import Layout, with_layout_constraint
 from jax.experimental import pallas as pl
 from jax.experimental.pallas import tpu as pltpu
 from jax.sharding import Mesh, PartitionSpec as P
@@ -28,7 +29,7 @@
     return lax.dot_general(a, b, (((1,), (1,)), ((), ())), preferred_element_type=jnp.float32)
 
 
-def pair_matmul_kernel(origin_ref, own_ref, other_ref, src_ref, out_ref, hi_ref, lo_ref):
+def pair_matmul_kernel(first_ref, origin_ref, own_ref, other_ref, src_ref, out_ref, hi_ref, lo_ref):
     blocks, _, half = own_ref.shape
     rows = out_ref.shape[1]
     origin = [origin_ref[comp : comp + 1, 0:1] for comp in range(3)]
@@ -50,7 +51,8 @@
                 hi_ref[j, :rows, cols] = hi
                 lo_ref[j, :rows, cols] = lo
 
-    src = [src_ref[:, comp : comp + 1] for comp in range(3)]
+    src_cols = src_ref[0].T
+    src = [src_cols[:, comp : comp + 1] for comp in range(3)]
     total = None
     for j in range(blocks):
         dist2 = None
@@ -70,26 +72,29 @@
     out_ref[0] = (0.5 * z).T
 
 
-def pair_matmul(origin, own, other, src_cols, peers):
+def pair_matmul(first, origin, own, other, src):
     blocks, height, half = own.shape
     rows = (height - TAIL) // 3
-    total_s = src_cols.shape[0]
-    per = total_s // peers
-    step = STEP
-    inner = per // step
-    pairs = total_s * 2 * half * blocks
+    peers, _, per = src.shape
+    pairs = peers * per * 2 * half * blocks
     return pl.pallas_call(
         pair_matmul_kernel,
         out_shape=jax.ShapeDtypeStruct((peers, rows, per), jnp.float32),
-        grid=(total_s // step,),
-        in_specs=[
-            pl.BlockSpec((8, half), lambda i: (0, 0)),
-            pl.BlockSpec((blocks, height, half), lambda i: (0, 0, 0)),
-            pl.BlockSpec((blocks, height, half), lambda i: (0, 0, 0)),
-            pl.BlockSpec((step, 8), lambda i: (i, 0)),
-        ],
-        out_specs=pl.BlockSpec((1, rows, step), lambda i: (i // inner, 0, i % inner)),
-        scratch_shapes=[pltpu.VMEM((blocks, 4 * rows, 2 * half), BF16)] * 2,
+        grid_spec=pltpu.PrefetchScalarGridSpec(
+            num_scalar_prefetch=1,
+            grid=(peers,),
+            in_specs=[
+                pl.BlockSpec((8, half), lambda i, f: (0, 0)),
+                pl.BlockSpec((blocks, height, half), lambda i, f: (0, 0, 0)),
+                pl.BlockSpec((blocks, height, half), lambda i, f: (0, 0, 0)),
+                pl.BlockSpec((1, 8, per), lambda i, f: (i, 0, 0)),
+            ],
+            out_specs=pl.BlockSpec((1, rows, per), lambda i, f: ((i + f[0]) % peers, 0, 0)),
+            scratch_shapes=[
+                pltpu.VMEM((blocks, 4 * rows, 2 * half), BF16),
+                pltpu.VMEM((blocks, 4 * rows, 2 * half), BF16),
+            ],
+        ),
         compiler_params=pltpu.CompilerParams(
             dimension_semantics=("arbitrary",), vmem_limit_bytes=32 * 1024 * 1024
         ),
@@ -98,10 +103,7 @@
             bytes_accessed=2 * blocks * height * half * 4 + peers * rows * per * 4,
             transcendentals=2 * pairs,
         ),
-    )(origin, own, other, src_cols)
-
-
-STEP = 512
+    )(first, origin, own, other, src)
 
 
 def body(tgt_coords, src_coords, src_values, grad_vectors):
@@ -120,26 +122,30 @@
     own = lax.all_to_all(load, ("y0", "h", "l"), 0, 0, tiled=True)
     other = lax.ppermute(own, "c", SWAP)
 
-    near = own[:, 3 * rows + 3 : 3 * rows + 6, :].reshape(n["y0"], 3 * nz, pts)
+    near = own[:, 3 * rows + 3 : 3 * rows + 6, :].reshape(n["y0"], nz, 3, pts)
     near = lax.dynamic_index_in_dim(near, lax.axis_index("y0"), 0, False)
-    near = jnp.pad(near, ((0, 4), (0, 0)))
-    src_all = lax.all_to_all(copies(near, n["yh"]), "yh", 0, 0, tiled=True)
-    src_all = src_all[:, : 3 * nz].reshape(n["yh"] * nz, 3, pts)
-    src_cols = src_all.transpose(0, 2, 1).reshape(n["yh"] * nz * pts, 3)
-    src_cols = jnp.pad(src_cols, ((0, 0), (0, 5)))
-    origin = jnp.mean(src_all, axis=(0, 2))
-    origin = jnp.broadcast_to(jnp.pad(origin, (0, 5))[:, None], (8, pts))
-    src_values, src_cols = lax.optimization_barrier((src_values, src_cols))
+    near = jnp.pad(near.transpose(1, 0, 2).reshape(3, nz * pts), ((0, 5), (0, 0)))
+    ny = n["yh"]
+    ring = [near]
+    for k in range(1, ny):
+        ring.append(lax.ppermute(near, "yh", [((i + k) % ny, i) for i in range(ny)]))
+    src = jnp.stack(ring)
+    first = lax.axis_index("yh").astype(jnp.int32).reshape(1)
+    origin = jnp.broadcast_to(jnp.mean(src, axis=(0, 2))[:, None], (8, pts))
+    src_values, src = lax.optimization_barrier((src_values, src))
 
-    values = lax.all_to_all(copies(src_values, nz), ("h", "l"), 0, 0, tiled=True)
+    rowmajor = Layout(major_to_minor=(0, 1, 2))
+    load = with_layout_constraint(copies(src_values, nz), rowmajor)
+    values = with_layout_constraint(lax.all_to_all(load, ("h", "l"), 0, 0, tiled=True), rowmajor)
 
-    partial_z = pair_matmul(origin, own, other, src_cols, n["yh"])
+    partial_z = pair_matmul(first, origin, own, other, src)
     spts = partial_z.shape[2]
     partial_z, values = lax.optimization_barrier((partial_z, values))
 
     arrived = lax.all_to_all(partial_z, "yh", 0, 0, tiled=True)
     z = arrived.sum(axis=0)
     z_all = lax.all_to_all(copies(z, nv), VEC, 0, 0, tiled=True).reshape(nv, n["c"], piece, spts)
+
     values = values.transpose(1, 0, 2).reshape(slab, spts)
 
     def product(core):

time: 137 us -> 137 us (level)
  starting transfers between devices: 21.3 us -> 35.2 us
  blocking collectives: 77.8 us -> 67.4 us
  local copies, waits for them, and re-layouts: 6.79 us -> 4.09 us
  matrix products: 2.85 us -> 0.77 us
    ppermute x0 -> x3, starting transfers between devices: none -> 13.9 us  [body(): lax.ppermute(near, 'yh', [((i + k) % ny, i) for i in range(ny)])]
    all_to_all x1 -> x0, blocking collectives: 12.6 us -> none  [body(): src_all = lax.all_to_all(copies(near, n['yh']), 'yh', 0, 0, tiled=True)]
    dot_general x2, matrix products: 2.85 us -> 0.77 us  [product(): lax.dot_general(zc, values, (((1,), (1,)), ((), ())), precision=lax.Preci...]
    all_to_all x1, blocking collectives: 15.4 us -> 16.9 us  [body(): arrived = lax.all_to_all(partial_z, 'yh', 0, 0, tiled=True)]
  transfers between devices with their start and end apart: 4 -> 7, of which waited for: 3 -> 3; matrix products, arithmetic and copies ran while one was open for 3% -> 1% of each run, Pallas kernels for 11% -> 11%
where the time goes in v5:
time: 137 us; the launch traced here: 136 us
  blocking collectives  67.4 us (49%)
  starting transfers between devices  35.2 us (26%)
  Pallas kernels  15.3 us (11%)
  waiting for transfers between devices  12.2 us (9%)
  local copies, waits for them, and re-layouts  4.09 us (3%)
    all_to_all x1, blocking collectives, body(): own = lax.all_to_all(load, ('y0', 'h', 'l'), 0, 0, tiled=True)  33.9 us
    all_to_all x1, blocking collectives, body(): arrived = lax.all_to_all(partial_z, 'yh', 0, 0, tiled=True)  16.9 us
    all_to_all x1, blocking collectives, body(): lax.all_to_all(part.reshape(nv, piece, slab), ('yh', 'y0'), 0, 0, tiled=T...  16.6 us
    pallas_call x1, Pallas kernels, pair_matmul(): pl.pallas_call(pair_matmul_kernel, out_shape=jax.ShapeDtypeStruct((peers,...  15.3 us
    ppermute x3, starting transfers between devices, body(): lax.ppermute(near, 'yh', [((i + k) % ny, i) for i in range(ny)])  13.9 us
    all_to_all x1, waiting for transfers between devices, body(): lax.all_to_all(copies(z, nv), VEC, 0, 0, tiled=True)  10.2 us
    ppermute x1, starting transfers between devices, body(): part = lax.ppermute(product(1 - c), 'c', SWAP) + product(c)  9.48 us
    ppermute x1, starting transfers between devices, body(): other = lax.ppermute(own, 'c', SWAP)  4.35 us
  transfers between devices with their start and end apart: 7, of which 3 were waited for; matrix products, arithmetic and copies ran while one was open for 1% of the time, Pallas kernels for 11%

profile of v5, /device:TPU:1, one launch (start us, length us, event | category | flops | bytes accessed | tf_op | source)
XLA Modules:
  0.0 136.3 jit_solution(6502096024651451578)
XLA Ops:
  0.0 0.0 copy-start.2
  0.0 1.0 copy.8
  1.0 0.0 copy-start.1
  1.1 0.1 pad.13.clone
  1.1 0.0 copy-done.2
  1.1 0.6 copy-done.1
  1.7 0.1 maximum_maximum_fusion
  1.8 0.1 broadcast_in_dim.14
  1.9 33.9 %all_to_all.25.own_ref = f32[8,200,128]{2,1,0:T(8,128)S(1)} all-to-all(f32[8,200,128]{2,1,0:T(8,128)S(1)} %bitcast.34), channel_id=1, replica_groups=mesh['yh'=4,'y0'=2,'h'=2,'l'=2,'c'=2,'x'=4,'zl'=2] {'y0','h','l'}, dimensions={0} | all-to-all | bytes 1638400 | tf_op jit(solution)/shard_map/all_to_all | solution.py:122
  35.8 4.3 %collective-permute-start.3 = (f32[8,200,128]{2,1,0:T(8,128)S(1)}, f32[8,200,128]{2,1,0:T(8,128)S(1)}, u32[]{:S(2)}, u32[]{:S(2)}) collective-permute-start(f32[8,200,128]{2,1,0:T(8,128)S(1)} %all_to_all.25.own_ref), channel_id=1, source_target_pairs={{0,8},{8,0},{1,9},{9,1},{2,10},{10,2},{3,11},{11,3},{4,12},{12,4},... | collective-permute-start | bytes 2457608 | tf_op jit(solution)/shard_map/ppermute | solution.py:123
  40.2 0.0 copy-start
  40.3 0.1 pad_bitcast_fusion
  40.4 6.5 %collective-permute-start.1 = (f32[8,512]{1,0:T(8,128)S(1)}, f32[8,512]{1,0:T(8,128)S(1)}, u32[]{:S(2)}, u32[]{:S(2)}) collective-permute-start(f32[8,512]{1,0:T(8,128)S(1)} %get-tuple-element.17), channel_id=1, source_target_pairs={{256,0},{384,128},{0,256},{128,384},{257,1},{385,129},{1,257},{129... | collective-permute-start | bytes 49160 | tf_op jit(solution)/shard_map/ppermute | solution.py:131
  46.9 2.4 %collective-permute-start.2 = (f32[8,512]{1,0:T(8,128)S(1)}, f32[8,512]{1,0:T(8,128)S(1)}, u32[]{:S(2)}, u32[]{:S(2)}) collective-permute-start(f32[8,512]{1,0:T(8,128)S(1)} %get-tuple-element.17), channel_id=1, source_target_pairs={{384,0},{0,128},{128,256},{256,384},{385,1},{1,129},{129,257},{257... | collective-permute-start | bytes 49160 | tf_op jit(solution)/shard_map/ppermute | solution.py:131
  49.4 5.0 %collective-permute-start = (f32[8,512]{1,0:T(8,128)S(1)}, f32[8,512]{1,0:T(8,128)S(1)}, u32[]{:S(2)}, u32[]{:S(2)}) collective-permute-start(f32[8,512]{1,0:T(8,128)S(1)} %get-tuple-element.17), channel_id=1, source_target_pairs={{128,0},{256,128},{384,256},{0,384},{129,1},{257,129},{385,257},{1... | collective-permute-start | bytes 49160 | tf_op jit(solution)/shard_map/ppermute | solution.py:131
  54.3 0.0 collective-permute-done.1
  54.4 0.0 collective-permute-done.2
  54.4 0.8 collective-permute-done
  55.2 0.0 copy-done
  55.2 0.8 broadcast_in_dim.16
  56.0 3.5 %all-to-all-start.1 = ((f32[4,256,128]{2,1,0:T(8,128)}), f32[4,256,128]{2,1,0:T(8,128)S(1)}, u32[]{:S(2)}, u32[]{:S(2)}) async-start(f32[4,256,128]{2,1,0:T(8,128)} %broadcast_in_dim.16), calls=%async_computation.1 | async-start | bytes 1048576 | tf_op jit(solution)/shard_map/all_to_all | solution.py:139
  59.5 0.1 reduce_sum.61
  59.6 0.1 reduce_sum.63
  59.7 0.1 reduce_sum.65
  59.9 0.0 collective-permute-done.3.other_ref
  59.9 0.1 broadcast_in_dim.15.origin_ref
  59.9 15.3 %shard_map.46 = f32[4,64,512]{2,1,0:T(8,128)S(1)} custom-call(s32[1]{0:T(128)} %bitcast.first_ref, f32[8,128]{1,0:T(8,128)S(1)} %broadcast_in_dim.15.origin_ref, f32[8,200,128]{2,1,0:T(8,128)S(1)} %all_to_all.25.own_ref, f32[8,200,128]{2,1,0:T(8,128)S(1)} %collective-permute-done.3.other_ref, f32[4,8,512]{2,1,0:T(8,128)S(1)} %pad_maximum_fusion.1.src_ref), custom_call_target="tpu_custom_call" | custom-call | flops 6442450944 | bytes 2162688 | tf_op jit(solution)/shard_map/pallas_call | solution.py:80
  75.2 0.0 all-to-all-done.1
  75.2 16.9 %all_to_all.26 = f32[4,64,512]{2,1,0:T(8,128)S(1)} all-to-all(f32[4,64,512]{2,1,0:T(8,128)S(1)} %shard_map.46), channel_id=1, replica_groups=mesh['yh'=4,'y0'=2,'h'=2,'l'=2,'c'=2,'x'=4,'zl'=2] {'yh'}, dimensions={0} | all-to-all | bytes 1048576 | tf_op jit(solution)/shard_map/all_to_all | solution.py:145
  92.1 1.1 broadcast_in_dim.17
  93.3 4.0 %all-to-all-start.3 = ((f32[8,64,512]{2,1,0:T(8,128)}), f32[8,64,512]{2,1,0:T(8,128)S(1)}, u32[]{:S(2)}, u32[]{:S(2)}) async-start(f32[8,64,512]{2,1,0:T(8,128)} %broadcast_in_dim.17), calls=%async_computation.3 | async-start | bytes 2097152 | tf_op jit(solution)/shard_map/all_to_all | solution.py:147
  97.2 0.2 copy.10
  97.4 10.2 %all-to-all-done.3 = f32[8,64,512]{2,1,0:T(8,128)S(1)} async-done(((f32[8,64,512]{2,1,0:T(8,128)}), f32[8,64,512]{2,1,0:T(8,128)S(1)}, u32[]{:S(2)}, u32[]{:S(2)}) %all-to-all-start.3) | async-done | bytes 1048608 | tf_op jit(solution)/shard_map/all_to_all | solution.py:147
  107.6 0.1 constant_dynamic-slice_fusion
  107.7 0.4 fusion
  108.1 9.5 %collective-permute-start.4 = (f32[256,256]{1,0:T(8,128)S(1)}, f32[256,256]{1,0:T(8,128)S(1)}, u32[]{:S(2)}, u32[]{:S(2)}) collective-permute-start(f32[256,256]{1,0:T(8,128)S(1)} %fusion), channel_id=1, source_target_pairs={{0,8},{8,0},{1,9},{9,1},{2,10},{10,2},{3,11},{11,3},{4,12},{12,4},... | collective-permute-start | bytes 786440 | tf_op jit(solution)/shard_map/ppermute | solution.py:155
  117.6 1.1 collective-permute-done.4
  118.7 0.4 convolution_add_fusion
  119.1 16.6 %all_to_all.27 = f32[8,32,256]{2,1,0:T(8,128)S(1)} all-to-all(f32[8,32,256]{2,1,0:T(8,128)S(1)} %bitcast.39), channel_id=1, replica_groups=mesh['yh'=4,'y0'=2,'h'=2,'l'=2,'c'=2,'x'=4,'zl'=2] {'yh','y0'}, dimensions={0} | all-to-all | bytes 524288 | tf_op jit(solution)/shard_map/all_to_all | solution.py:156
  135.7 0.6 reduce_sum.68
  (10 shorter events, 0.1 us)
Async XLA Ops:
  0.0 1.1 copy-start.2
  1.0 0.7 copy-start.1
  35.8 24.0 %collective-permute-start.3 = (f32[8,200,128]{2,1,0:T(8,128)S(1)}, f32[8,200,128]{2,1,0:T(8,128)S(1)}, u32[]{:S(2)}, u32[]{:S(2)}) collective-permute-start(f32[8,200,128]{2,1,0:T(8,128)S(1)} %all_to_all.25.own_ref), channel_id=1, source_target_pairs={{0,8},{8,0},{1,9},{9,1},{2,10},{10,2},{3,11},{11,3},{4,12},{12,4},... | collective-permute-start | bytes 2457608 | tf_op jit(solution)/shard_map/ppermute | solution.py:123
  40.2 15.0 %copy-start = (f32[256,128]{1,0:T(8,128)S(1)}, f32[256,128]{1,0:T(8,128)}, u32[]{:S(2)}) copy-start(f32[256,128]{1,0:T(8,128)} %param.6) | copy-start | bytes 393220
  40.4 14.0 %collective-permute-start.1 = (f32[8,512]{1,0:T(8,128)S(1)}, f32[8,512]{1,0:T(8,128)S(1)}, u32[]{:S(2)}, u32[]{:S(2)}) collective-permute-start(f32[8,512]{1,0:T(8,128)S(1)} %get-tuple-element.17), channel_id=1, source_target_pairs={{256,0},{384,128},{0,256},{128,384},{257,1},{385,129},{1,257},{129... | collective-permute-start | bytes 49160 | tf_op jit(solution)/shard_map/ppermute | solution.py:131
  46.9 7.4 %collective-permute-start.2 = (f32[8,512]{1,0:T(8,128)S(1)}, f32[8,512]{1,0:T(8,128)S(1)}, u32[]{:S(2)}, u32[]{:S(2)}) collective-permute-start(f32[8,512]{1,0:T(8,128)S(1)} %get-tuple-element.17), channel_id=1, source_target_pairs={{384,0},{0,128},{128,256},{256,384},{385,1},{1,129},{129,257},{257... | collective-permute-start | bytes 49160 | tf_op jit(solution)/shard_map/ppermute | solution.py:131
  49.4 5.8 %collective-permute-start = (f32[8,512]{1,0:T(8,128)S(1)}, f32[8,512]{1,0:T(8,128)S(1)}, u32[]{:S(2)}, u32[]{:S(2)}) collective-permute-start(f32[8,512]{1,0:T(8,128)S(1)} %get-tuple-element.17), channel_id=1, source_target_pairs={{128,0},{256,128},{384,256},{0,384},{129,1},{257,129},{385,257},{1... | collective-permute-start | bytes 49160 | tf_op jit(solution)/shard_map/ppermute | solution.py:131
  56.0 19.2 %all-to-all-start.1 = ((f32[4,256,128]{2,1,0:T(8,128)}), f32[4,256,128]{2,1,0:T(8,128)S(1)}, u32[]{:S(2)}, u32[]{:S(2)}) async-start(f32[4,256,128]{2,1,0:T(8,128)} %broadcast_in_dim.16), calls=%async_computation.1 | async-start | bytes 1048576 | tf_op jit(solution)/shard_map/all_to_all | solution.py:139
  93.3 14.3 %all-to-all-start.3 = ((f32[8,64,512]{2,1,0:T(8,128)}), f32[8,64,512]{2,1,0:T(8,128)S(1)}, u32[]{:S(2)}, u32[]{:S(2)}) async-start(f32[8,64,512]{2,1,0:T(8,128)} %broadcast_in_dim.17), calls=%async_computation.3 | async-start | bytes 2097152 | tf_op jit(solution)/shard_map/all_to_all | solution.py:147
  108.1 10.6 %collective-permute-start.4 = (f32[256,256]{1,0:T(8,128)S(1)}, f32[256,256]{1,0:T(8,128)S(1)}, u32[]{:S(2)}, u32[]{:S(2)}) collective-permute-start(f32[256,256]{1,0:T(8,128)S(1)} %fusion), channel_id=1, source_target_pairs={{0,8},{8,0},{1,9},{9,1},{2,10},{10,2},{3,11},{11,3},{4,12},{12,4},... | collective-permute-start | bytes 786440 | tf_op jit(solution)/shard_map/ppermute | solution.py:155

commit v6 on v5

--- a/solution.py
+++ b/solution.py
@@ -13,7 +13,7 @@
 VEC = ("x", "zl")
 SWAP = [(0, 1), (1, 0)]
 BF16 = jnp.bfloat16
-TAIL = 8
+TAIL = 16
 
 
 def copies(block, peers):
@@ -29,7 +29,7 @@
     return lax.dot_general(a, b, (((1,), (1,)), ((), ())), preferred_element_type=jnp.float32)
 
 
-def pair_matmul_kernel(first_ref, origin_ref, own_ref, other_ref, src_ref, out_ref, hi_ref, lo_ref):
+def pair_matmul_kernel(origin_ref, own_ref, other_ref, src_ref, out_ref, hi_ref, lo_ref):
     blocks, _, half = own_ref.shape
     rows = out_ref.shape[1]
     origin = [origin_ref[comp : comp + 1, 0:1] for comp in range(3)]
@@ -72,7 +72,7 @@
     out_ref[0] = (0.5 * z).T
 
 
-def pair_matmul(first, origin, own, other, src):
+def pair_matmul(origin, own, other, src):
     blocks, height, half = own.shape
     rows = (height - TAIL) // 3
     peers, _, per = src.shape
@@ -80,21 +80,10 @@
     return pl.pallas_call(
         pair_matmul_kernel,
         out_shape=jax.ShapeDtypeStruct((peers, rows, per), jnp.float32),
-        grid_spec=pltpu.PrefetchScalarGridSpec(
-            num_scalar_prefetch=1,
-            grid=(peers,),
-            in_specs=[
-                pl.BlockSpec((8, half), lambda i, f: (0, 0)),
-                pl.BlockSpec((blocks, height, half), lambda i, f: (0, 0, 0)),
-                pl.BlockSpec((blocks, height, half), lambda i, f: (0, 0, 0)),
-                pl.BlockSpec((1, 8, per), lambda i, f: (i, 0, 0)),
-            ],
-            out_specs=pl.BlockSpec((1, rows, per), lambda i, f: ((i + f[0]) % peers, 0, 0)),
-            scratch_shapes=[
-                pltpu.VMEM((blocks, 4 * rows, 2 * half), BF16),
-                pltpu.VMEM((blocks, 4 * rows, 2 * half), BF16),
-            ],
-        ),
+        grid=(peers,),
+        in_specs=[pl.BlockSpec(memory_space=pltpu.VMEM)] * 3 + [pl.BlockSpec((1, 8, per), lambda i: (i, 0, 0))],
+        out_specs=pl.BlockSpec((1, rows, per), lambda i: (i, 0, 0)),
+        scratch_shapes=[pltpu.VMEM((blocks, 4 * rows, 2 * half), BF16)] * 2,
         compiler_params=pltpu.CompilerParams(
             dimension_semantics=("arbitrary",), vmem_limit_bytes=32 * 1024 * 1024
         ),
@@ -103,7 +92,7 @@
             bytes_accessed=2 * blocks * height * half * 4 + peers * rows * per * 4,
             transcendentals=2 * pairs,
         ),
-    )(first, origin, own, other, src)
+    )(origin, own, other, src)
 
 
 def body(tgt_coords, src_coords, src_values, grad_vectors):
@@ -115,37 +104,34 @@
     piece = rows // n["c"]
     c = lax.axis_index("c")
 
+    src_y = lax.all_to_all(copies(src_coords, n["yh"]), "yh", 0, 0, tiled=True)
+    src_y = src_y.reshape(3 * n["yh"], pts)
+    rowmajor = Layout(major_to_minor=(0, 1, 2))
+    values = with_layout_constraint(copies(src_values, nz), rowmajor)
+
     grads = grad_vectors.reshape(3, nz, rows, pts).transpose(1, 0, 2, 3).reshape(nz, 3 * rows, pts)
-    tail = jnp.concatenate([tgt_coords, src_coords, jnp.zeros((TAIL - 6, pts), jnp.float32)], axis=0)
+    tail = jnp.concatenate([tgt_coords, src_y, jnp.zeros((1, pts), jnp.float32)], axis=0)
     load = jnp.concatenate([grads, copies(tail, nz)], axis=1)
     load = copies(load, n["y0"]).reshape(n["y0"] * nz, 3 * rows + TAIL, pts)
     own = lax.all_to_all(load, ("y0", "h", "l"), 0, 0, tiled=True)
+    values, own = lax.optimization_barrier((values, own))
     other = lax.ppermute(own, "c", SWAP)
 
-    near = own[:, 3 * rows + 3 : 3 * rows + 6, :].reshape(n["y0"], nz, 3, pts)
+    near = own[:, 3 * rows + 3 : 3 * rows + 3 + 3 * n["yh"], :].reshape(n["y0"], nz, n["yh"], 3, pts)
     near = lax.dynamic_index_in_dim(near, lax.axis_index("y0"), 0, False)
-    near = jnp.pad(near.transpose(1, 0, 2).reshape(3, nz * pts), ((0, 5), (0, 0)))
-    ny = n["yh"]
-    ring = [near]
-    for k in range(1, ny):
-        ring.append(lax.ppermute(near, "yh", [((i + k) % ny, i) for i in range(ny)]))
-    src = jnp.stack(ring)
-    first = lax.axis_index("yh").astype(jnp.int32).reshape(1)
+    src = near.transpose(1, 2, 0, 3).reshape(n["yh"], 3, nz * pts)
+    src = jnp.pad(src, ((0, 0), (0, 5), (0, 0)))
     origin = jnp.broadcast_to(jnp.mean(src, axis=(0, 2))[:, None], (8, pts))
-    src_values, src = lax.optimization_barrier((src_values, src))
 
-    rowmajor = Layout(major_to_minor=(0, 1, 2))
-    load = with_layout_constraint(copies(src_values, nz), rowmajor)
-    values = with_layout_constraint(lax.all_to_all(load, ("h", "l"), 0, 0, tiled=True), rowmajor)
+    values = with_layout_constraint(lax.all_to_all(values, ("h", "l"), 0, 0, tiled=True), rowmajor)
 
-    partial_z = pair_matmul(first, origin, own, other, src)
+    partial_z = pair_matmul(origin, own, other, src)
     spts = partial_z.shape[2]
     partial_z, values = lax.optimization_barrier((partial_z, values))
 
     arrived = lax.all_to_all(partial_z, "yh", 0, 0, tiled=True)
     z = arrived.sum(axis=0)
     z_all = lax.all_to_all(copies(z, nv), VEC, 0, 0, tiled=True).reshape(nv, n["c"], piece, spts)
-
     values = values.transpose(1, 0, 2).reshape(slab, spts)
 
     def product(core):

time: 137 us -> 132 us (0.964)
  starting transfers between devices: 35.2 us -> 29.8 us
  waiting for transfers between devices: 12.2 us -> 17.3 us
  blocking collectives: 67.4 us -> 62.9 us
    ppermute x3 -> x0, starting transfers between devices: 13.9 us -> none  [body(): lax.ppermute(near, 'yh', [((i + k) % ny, i) for i in range(ny)])]
    all_to_all x1 -> x2, starting transfers between devices: 3.47 us -> 11.1 us  [the longest x1 7.63 us: body(): src_y = lax.all_to_all(copies(src_coords, n['yh']), 'yh', 0, 0, tiled=True)]
    all_to_all x1 -> x2, waiting for transfers between devices: 0.01 us -> 5.48 us  [the longest x1 5.48 us: body(): src_y = lax.all_to_all(copies(src_coords, n['yh']), 'yh', 0, 0, tiled=True)]
    all_to_all x1, blocking collectives: 16.9 us -> 14.2 us  [body(): arrived = lax.all_to_all(partial_z, 'yh', 0, 0, tiled=True)]
    all_to_all x1, starting transfers between devices: 3.96 us -> 5.84 us  [body(): lax.all_to_all(copies(z, nv), VEC, 0, 0, tiled=True)]
    ppermute x1, starting transfers between devices: 9.48 us -> 8.1 us  [body(): part = lax.ppermute(product(1 - c), 'c', SWAP) + product(c)]
    all_to_all x1, blocking collectives: 33.9 us -> 32.6 us  [body(): own = lax.all_to_all(load, ('y0', 'h', 'l'), 0, 0, tiled=True)]
    broadcast_in_dim x4 -> x5, local copies, waits for them, and re-layouts: 2 us -> 3.26 us  [copies(): return jnp.broadcast_to(block[None], (peers,) + block.shape)]
  transfers between devices with their start and end apart: 7 -> 5, of which waited for: 3 -> 3; matrix products, arithmetic and copies ran while one was open for 1% -> 1% of each run, Pallas kernels for 11% -> 12%
where the time goes in v6:
time: 132 us
  blocking collectives  62.9 us (48%)
  starting transfers between devices  29.8 us (23%)
  waiting for transfers between devices  17.3 us (13%)
  Pallas kernels  15.3 us (12%)
  local copies, waits for them, and re-layouts  4.8 us (4%)
    all_to_all x1, blocking collectives, body(): own = lax.all_to_all(load, ('y0', 'h', 'l'), 0, 0, tiled=True)  32.6 us
    all_to_all x1, blocking collectives, body(): lax.all_to_all(part.reshape(nv, piece, slab), ('yh', 'y0'), 0, 0, tiled=T...  16.1 us
    pallas_call x1, Pallas kernels, pair_matmul(): pl.pallas_call(pair_matmul_kernel, out_shape=jax.ShapeDtypeStruct((peers,...  15.3 us
    all_to_all x1, blocking collectives, body(): arrived = lax.all_to_all(partial_z, 'yh', 0, 0, tiled=True)  14.2 us
    all_to_all x1, waiting for transfers between devices, body(): lax.all_to_all(copies(z, nv), VEC, 0, 0, tiled=True)  10.6 us
    ppermute x1, starting transfers between devices, body(): part = lax.ppermute(product(1 - c), 'c', SWAP) + product(c)  8.1 us
    all_to_all x1, starting transfers between devices, body(): src_y = lax.all_to_all(copies(src_coords, n['yh']), 'yh', 0, 0, tiled=True)  7.63 us
    all_to_all x1, starting transfers between devices, body(): lax.all_to_all(copies(z, nv), VEC, 0, 0, tiled=True)  5.84 us
  transfers between devices with their start and end apart: 5, of which 3 were waited for; matrix products, arithmetic and copies ran while one was open for 1% of the time, Pallas kernels for 12%

profile of v6, /device:TPU:1, one launch (start us, length us, event | category | flops | bytes accessed | tf_op | source)
XLA Modules:
  0.0 131.9 jit_solution(2724602998672981542)
XLA Ops:
  0.0 1.3 broadcast_in_dim.15
  1.3 7.6 %all-to-all-start = ((f32[4,3,128]{2,1,0:T(4,128)}), f32[4,3,128]{2,1,0:T(4,128)S(1)}, u32[]{:S(2)}, u32[]{:S(2)}) async-start(f32[4,3,128]{2,1,0:T(4,128)} %broadcast_in_dim.15), calls=%async_computation | async-start | bytes 16384 | tf_op jit(solution)/shard_map/all_to_all | solution.py:107
  8.9 1.0 copy.9
  9.9 0.1 pad.9.clone
  10.0 0.0 copy-start.1
  10.0 5.5 %all-to-all-done = f32[4,3,128]{2,1,0:T(4,128)S(1)} async-done(((f32[4,3,128]{2,1,0:T(4,128)}), f32[4,3,128]{2,1,0:T(4,128)S(1)}, u32[]{:S(2)}, u32[]{:S(2)}) %all-to-all-start) | async-done | bytes 6176 | tf_op jit(solution)/shard_map/all_to_all | solution.py:107
  15.5 0.0 copy-done.1
  15.5 0.1 maximum_maximum_fusion
  15.6 0.1 broadcast_in_dim.18
  15.7 0.0 copy-start
  15.7 32.6 %all_to_all.30.own_ref = f32[8,208,128]{2,1,0:T(8,128)S(1)} all-to-all(f32[8,208,128]{2,1,0:T(8,128)S(1)} %bitcast.24), channel_id=1, replica_groups=mesh['yh'=4,'y0'=2,'h'=2,'l'=2,'c'=2,'x'=4,'zl'=2] {'y0','h','l'}, dimensions={0} | all-to-all | bytes 1703936 | tf_op jit(solution)/shard_map/all_to_all | solution.py:116
  48.3 0.0 copy-done
  48.3 0.8 broadcast_in_dim.14
  49.1 4.8 %collective-permute-start = (f32[8,208,128]{2,1,0:T(8,128)S(1)}, f32[8,208,128]{2,1,0:T(8,128)S(1)}, u32[]{:S(2)}, u32[]{:S(2)}) collective-permute-start(f32[8,208,128]{2,1,0:T(8,128)S(1)} %all_to_all.30.own_ref), channel_id=1, source_target_pairs={{0,8},{8,0},{1,9},{9,1},{2,10},{10,2},{3,11},{11,3},{4,12},{12,4},... | collective-permute-start | bytes 2555912 | tf_op jit(solution)/shard_map/ppermute | solution.py:118
  54.0 3.5 %all-to-all-start.2 = ((f32[4,256,128]{2,1,0:T(8,128)}), f32[4,256,128]{2,1,0:T(8,128)S(1)}, u32[]{:S(2)}, u32[]{:S(2)}) async-start(f32[4,256,128]{2,1,0:T(8,128)} %broadcast_in_dim.14), calls=%async_computation.2 | async-start | bytes 1048576 | tf_op jit(solution)/shard_map/all_to_all | solution.py:126
  57.5 0.1 fusion
  57.6 0.0 collective-permute-done.other_ref
  57.6 0.1 broadcast_in_dim.19.origin_ref
  57.7 15.3 %shard_map.46 = f32[4,64,512]{2,1,0:T(8,128)S(1)} custom-call(f32[8,128]{1,0:T(8,128)S(1)} %broadcast_in_dim.19.origin_ref, f32[8,208,128]{2,1,0:T(8,128)S(1)} %all_to_all.30.own_ref, f32[8,208,128]{2,1,0:T(8,128)S(1)} %collective-permute-done.other_ref, f32[4,8,512]{2,1,0:T(8,128)S(1)} %get-tuple-element.15.src_ref), custom_call_target="tpu_custom_call" | custom-call | flops 6442450944 | bytes 2228224 | tf_op jit(solution)/shard_map/pallas_call | solution.py:80
  73.0 0.0 all-to-all-done.2
  73.0 14.2 %all_to_all.31 = f32[4,64,512]{2,1,0:T(8,128)S(1)} all-to-all(f32[4,64,512]{2,1,0:T(8,128)S(1)} %shard_map.46), channel_id=1, replica_groups=mesh['yh'=4,'y0'=2,'h'=2,'l'=2,'c'=2,'x'=4,'zl'=2] {'yh'}, dimensions={0} | all-to-all | bytes 1048576 | tf_op jit(solution)/shard_map/all_to_all | solution.py:132
  87.2 1.1 broadcast_in_dim.20
  88.3 5.8 %all-to-all-start.4 = ((f32[8,64,512]{2,1,0:T(8,128)}), f32[8,64,512]{2,1,0:T(8,128)S(1)}, u32[]{:S(2)}, u32[]{:S(2)}) async-start(f32[8,64,512]{2,1,0:T(8,128)} %broadcast_in_dim.20), calls=%async_computation.4 | async-start | bytes 2097152 | tf_op jit(solution)/shard_map/all_to_all | solution.py:134
  94.2 0.2 copy.14
  94.4 10.6 %all-to-all-done.4 = f32[8,64,512]{2,1,0:T(8,128)S(1)} async-done(((f32[8,64,512]{2,1,0:T(8,128)}), f32[8,64,512]{2,1,0:T(8,128)S(1)}, u32[]{:S(2)}, u32[]{:S(2)}) %all-to-all-start.4) | async-done | bytes 1048608 | tf_op jit(solution)/shard_map/all_to_all | solution.py:134
  105.0 0.1 constant_dynamic-slice_fusion
  105.1 0.4 fusion.1
  105.5 8.1 %collective-permute-start.1 = (f32[256,256]{1,0:T(8,128)S(1)}, f32[256,256]{1,0:T(8,128)S(1)}, u32[]{:S(2)}, u32[]{:S(2)}) collective-permute-start(f32[256,256]{1,0:T(8,128)S(1)} %fusion.1), channel_id=1, source_target_pairs={{0,8},{8,0},{1,9},{9,1},{2,10},{10,2},{3,11},{11,3},{4,12},{12,4},... | collective-permute-start | bytes 786440 | tf_op jit(solution)/shard_map/ppermute | solution.py:141
  113.6 1.1 collective-permute-done.1
  114.8 0.4 convolution_add_fusion
  115.1 16.1 %all_to_all.32 = f32[8,32,256]{2,1,0:T(8,128)S(1)} all-to-all(f32[8,32,256]{2,1,0:T(8,128)S(1)} %bitcast.29), channel_id=1, replica_groups=mesh['yh'=4,'y0'=2,'h'=2,'l'=2,'c'=2,'x'=4,'zl'=2] {'yh','y0'}, dimensions={0} | all-to-all | bytes 524288 | tf_op jit(solution)/shard_map/all_to_all | solution.py:142
  131.3 0.6 reduce_sum.29
  (9 shorter events, 0.2 us)
Async XLA Ops:
  1.3 14.2 %all-to-all-start = ((f32[4,3,128]{2,1,0:T(4,128)}), f32[4,3,128]{2,1,0:T(4,128)S(1)}, u32[]{:S(2)}, u32[]{:S(2)}) async-start(f32[4,3,128]{2,1,0:T(4,128)} %broadcast_in_dim.15), calls=%async_computation | async-start | bytes 16384 | tf_op jit(solution)/shard_map/all_to_all | solution.py:107
  10.0 5.5 %copy-start.1 = (f32[3,128]{1,0:T(4,128)S(1)}, f32[3,128]{1,0:T(4,128)}, u32[]{:S(2)}) copy-start(f32[3,128]{1,0:T(4,128)} %param.4) | copy-start | bytes 4612
  15.7 32.6 %copy-start = (f32[256,128]{1,0:T(8,128)S(1)}, f32[256,128]{1,0:T(8,128)}, u32[]{:S(2)}) copy-start(f32[256,128]{1,0:T(8,128)} %param.6) | copy-start | bytes 393220
  49.1 8.5 %collective-permute-start = (f32[8,208,128]{2,1,0:T(8,128)S(1)}, f32[8,208,128]{2,1,0:T(8,128)S(1)}, u32[]{:S(2)}, u32[]{:S(2)}) collective-permute-start(f32[8,208,128]{2,1,0:T(8,128)S(1)} %all_to_all.30.own_ref), channel_id=1, source_target_pairs={{0,8},{8,0},{1,9},{9,1},{2,10},{10,2},{3,11},{11,3},{4,12},{12,4},... | collective-permute-start | bytes 2555912 | tf_op jit(solution)/shard_map/ppermute | solution.py:118
  54.0 19.0 %all-to-all-start.2 = ((f32[4,256,128]{2,1,0:T(8,128)}), f32[4,256,128]{2,1,0:T(8,128)S(1)}, u32[]{:S(2)}, u32[]{:S(2)}) async-start(f32[4,256,128]{2,1,0:T(8,128)} %broadcast_in_dim.14), calls=%async_computation.2 | async-start | bytes 1048576 | tf_op jit(solution)/shard_map/all_to_all | solution.py:126
  88.3 16.7 %all-to-all-start.4 = ((f32[8,64,512]{2,1,0:T(8,128)}), f32[8,64,512]{2,1,0:T(8,128)S(1)}, u32[]{:S(2)}, u32[]{:S(2)}) async-start(f32[8,64,512]{2,1,0:T(8,128)} %broadcast_in_dim.20), calls=%async_computation.4 | async-start | bytes 2097152 | tf_op jit(solution)/shard_map/all_to_all | solution.py:134
  105.5 9.2 %collective-permute-start.1 = (f32[256,256]{1,0:T(8,128)S(1)}, f32[256,256]{1,0:T(8,128)S(1)}, u32[]{:S(2)}, u32[]{:S(2)}) collective-permute-start(f32[256,256]{1,0:T(8,128)S(1)} %fusion.1), channel_id=1, source_target_pairs={{0,8},{8,0},{1,9},{9,1},{2,10},{10,2},{3,11},{11,3},{4,12},{12,4},... | collective-permute-start | bytes 786440 | tf_op jit(solution)/shard_map/ppermute | solution.py:141

commit v7 on v6

--- a/solution.py
+++ b/solution.py
@@ -127,18 +127,19 @@
 
     partial_z = pair_matmul(origin, own, other, src)
     spts = partial_z.shape[2]
-    partial_z, values = lax.optimization_barrier((partial_z, values))
+    values = values.transpose(1, 0, 2).reshape(slab, spts)
+    partial_z, values, south = lax.optimization_barrier((partial_z, values, c == 0))
 
     arrived = lax.all_to_all(partial_z, "yh", 0, 0, tiled=True)
-    z = arrived.sum(axis=0)
+    z = arrived.sum(axis=0).reshape(n["c"], piece, spts)
+    z = jnp.where(south, z, z[::-1]).reshape(rows, spts)
     z_all = lax.all_to_all(copies(z, nv), VEC, 0, 0, tiled=True).reshape(nv, n["c"], piece, spts)
-    values = values.transpose(1, 0, 2).reshape(slab, spts)
 
-    def product(core):
-        zc = lax.dynamic_index_in_dim(z_all, core, 1, False).reshape(nv * piece, spts)
+    def product(k):
+        zc = z_all[:, k].reshape(nv * piece, spts)
         return lax.dot_general(zc, values, (((1,), (1,)), ((), ())), precision=lax.Precision.HIGH)
 
-    part = lax.ppermute(product(1 - c), "c", SWAP) + product(c)
+    part = lax.ppermute(product(1), "c", SWAP) + product(0)
     back = lax.all_to_all(part.reshape(nv, piece, slab), ("yh", "y0"), 0, 0, tiled=True)
     return back.sum(axis=0)
 

time: 132 us -> 147 us (1.11)
  blocking collectives: 62.9 us -> 81.8 us
  starting transfers between devices: 29.8 us -> 21.8 us
  waiting for transfers between devices: 17.3 us -> 21.6 us
    all_to_all x0 -> x1, blocking collectives: none -> 16.5 us  [body(): lax.all_to_all(copies(z, nv), VEC, 0, 0, tiled=True)]
    all_to_all x1, waiting for transfers between devices: 0.01 us -> 15 us  [body(): lax.all_to_all(values, ('h', 'l'), 0, 0, tiled=True)]
    all_to_all x1 -> x0, waiting for transfers between devices: 10.6 us -> none  [body(): lax.all_to_all(copies(z, nv), VEC, 0, 0, tiled=True)]
    all_to_all x1 -> x0, starting transfers between devices: 5.84 us -> none  [body(): lax.all_to_all(copies(z, nv), VEC, 0, 0, tiled=True)]
    all_to_all x1, blocking collectives: 14.2 us -> 17 us  [body(): arrived = lax.all_to_all(partial_z, 'yh', 0, 0, tiled=True)]
    ppermute x1, starting transfers between devices: 8.1 us -> 5.92 us  [body(): part = lax.ppermute(product(1), 'c', SWAP) + product(0)]
  transfers between devices with their start and end apart: 5 -> 4, of which waited for: 3 -> 3; matrix products, arithmetic and copies ran while one was open for 1% -> 1% of each run, Pallas kernels for 12% -> 0%
where the time goes in v7:
time: 147 us; the launch traced here: 146 us
  blocking collectives  81.8 us (56%)
  starting transfers between devices  21.8 us (15%)
  waiting for transfers between devices  21.6 us (15%)
  Pallas kernels  15.3 us (10%)
  local copies, waits for them, and re-layouts  3.8 us (3%)
    all_to_all x1, blocking collectives, body(): own = lax.all_to_all(load, ('y0', 'h', 'l'), 0, 0, tiled=True)  32.6 us
    all_to_all x1, blocking collectives, body(): arrived = lax.all_to_all(partial_z, 'yh', 0, 0, tiled=True)  17 us
    all_to_all x1, blocking collectives, body(): lax.all_to_all(copies(z, nv), VEC, 0, 0, tiled=True)  16.5 us
    all_to_all x1, blocking collectives, body(): lax.all_to_all(part.reshape(nv, piece, slab), ('yh', 'y0'), 0, 0, tiled=T...  15.8 us
    pallas_call x1, Pallas kernels, pair_matmul(): pl.pallas_call(pair_matmul_kernel, out_shape=jax.ShapeDtypeStruct((peers,...  15.3 us
    all_to_all x1, waiting for transfers between devices, body(): lax.all_to_all(values, ('h', 'l'), 0, 0, tiled=True)  15 us
    all_to_all x1, starting transfers between devices, body(): src_y = lax.all_to_all(copies(src_coords, n['yh']), 'yh', 0, 0, tiled=True)  7.63 us
    ppermute x1, starting transfers between devices, body(): part = lax.ppermute(product(1), 'c', SWAP) + product(0)  5.92 us
  transfers between devices with their start and end apart: 4, of which 3 were waited for; matrix products, arithmetic and copies ran while one was open for 1% of the time, Pallas kernels for 0%

profile of v7, /device:TPU:1, one launch (start us, length us, event | category | flops | bytes accessed | tf_op | source)
XLA Modules:
  0.0 146.2 jit_solution(817622015069782166)
XLA Ops:
  0.0 1.3 broadcast_in_dim.17
  1.3 7.6 %all-to-all-start = ((f32[4,3,128]{2,1,0:T(4,128)}), f32[4,3,128]{2,1,0:T(4,128)S(1)}, u32[]{:S(2)}, u32[]{:S(2)}) async-start(f32[4,3,128]{2,1,0:T(4,128)} %broadcast_in_dim.17), calls=%async_computation | async-start | bytes 16384 | tf_op jit(solution)/shard_map/all_to_all | solution.py:107
  8.9 1.0 copy.9
  9.9 0.1 pad.9.clone
  10.0 0.0 copy-start.1
  10.0 5.5 %all-to-all-done = f32[4,3,128]{2,1,0:T(4,128)S(1)} async-done(((f32[4,3,128]{2,1,0:T(4,128)}), f32[4,3,128]{2,1,0:T(4,128)S(1)}, u32[]{:S(2)}, u32[]{:S(2)}) %all-to-all-start) | async-done | bytes 6176 | tf_op jit(solution)/shard_map/all_to_all | solution.py:107
  15.5 0.0 copy-done.1
  15.5 0.1 maximum_maximum_fusion
  15.6 0.1 broadcast_in_dim.20
  15.7 0.0 copy-start
  15.7 32.6 %all_to_all.30.own_ref = f32[8,208,128]{2,1,0:T(8,128)S(1)} all-to-all(f32[8,208,128]{2,1,0:T(8,128)S(1)} %bitcast.26), channel_id=1, replica_groups=mesh['yh'=4,'y0'=2,'h'=2,'l'=2,'c'=2,'x'=4,'zl'=2] {'y0','h','l'}, dimensions={0} | all-to-all | bytes 1703936 | tf_op jit(solution)/shard_map/all_to_all | solution.py:116
  48.3 0.0 copy-done
  48.3 0.8 broadcast_in_dim.16
  49.1 4.8 %collective-permute-start = (f32[8,208,128]{2,1,0:T(8,128)S(1)}, f32[8,208,128]{2,1,0:T(8,128)S(1)}, u32[]{:S(2)}, u32[]{:S(2)}) collective-permute-start(f32[8,208,128]{2,1,0:T(8,128)S(1)} %all_to_all.30.own_ref), channel_id=1, source_target_pairs={{0,8},{8,0},{1,9},{9,1},{2,10},{10,2},{3,11},{11,3},{4,12},{12,4},... | collective-permute-start | bytes 2555912 | tf_op jit(solution)/shard_map/ppermute | solution.py:118
  53.9 3.5 %all-to-all-start.2 = ((f32[4,256,128]{2,1,0:T(8,128)}), f32[4,256,128]{2,1,0:T(8,128)S(1)}, u32[]{:S(2)}, u32[]{:S(2)}) async-start(f32[4,256,128]{2,1,0:T(8,128)} %broadcast_in_dim.16), calls=%async_computation.2 | async-start | bytes 1048576 | tf_op jit(solution)/shard_map/all_to_all | solution.py:126
  57.5 0.1 fusion.1
  57.6 15.0 %all-to-all-done.2 = f32[4,256,128]{2,1,0:T(8,128)S(1)} async-done(((f32[4,256,128]{2,1,0:T(8,128)}), f32[4,256,128]{2,1,0:T(8,128)S(1)}, u32[]{:S(2)}, u32[]{:S(2)}) %all-to-all-start.2) | async-done | bytes 524320 | tf_op jit(solution)/shard_map/all_to_all | solution.py:126
  72.6 0.2 copy.14
  72.8 0.0 collective-permute-done.other_ref
  72.8 0.1 broadcast_in_dim.21.origin_ref
  72.9 15.3 %shard_map.46 = f32[4,64,512]{2,1,0:T(8,128)S(1)} custom-call(f32[8,128]{1,0:T(8,128)S(1)} %broadcast_in_dim.21.origin_ref, f32[8,208,128]{2,1,0:T(8,128)S(1)} %all_to_all.30.own_ref, f32[8,208,128]{2,1,0:T(8,128)S(1)} %collective-permute-done.other_ref, f32[4,8,512]{2,1,0:T(8,128)S(1)} %get-tuple-element.17.src_ref), custom_call_target="tpu_custom_call" | custom-call | flops 6442450944 | bytes 2228224 | tf_op jit(solution)/shard_map/pallas_call | solution.py:80
  88.2 17.0 %all_to_all.31 = f32[4,64,512]{2,1,0:T(8,128)S(1)} all-to-all(f32[4,64,512]{2,1,0:T(8,128)S(1)} %shard_map.46), channel_id=1, replica_groups=mesh['yh'=4,'y0'=2,'h'=2,'l'=2,'c'=2,'x'=4,'zl'=2] {'yh'}, dimensions={0} | all-to-all | bytes 1048576 | tf_op jit(solution)/shard_map/all_to_all | solution.py:133
  105.2 0.1 broadcast_in_dim.23
  105.4 16.5 %all_to_all.32 = f32[8,64,512]{2,1,0:T(8,128)S(1)} all-to-all(f32[8,64,512]{2,1,0:T(8,128)S(1)} %broadcast_in_dim.23), channel_id=1, replica_groups=mesh['yh'=4,'y0'=2,'h'=2,'l'=2,'c'=2,'x'=4,'zl'=2] {'x','zl'}, dimensions={0} | all-to-all | bytes 2097152 | tf_op jit(solution)/shard_map/all_to_all | solution.py:136
  121.8 0.1 fusion
  121.9 0.4 fusion.2
  122.3 5.9 %collective-permute-start.1 = (f32[256,256]{1,0:T(8,128)S(1)}, f32[256,256]{1,0:T(8,128)S(1)}, u32[]{:S(2)}, u32[]{:S(2)}) collective-permute-start(f32[256,256]{1,0:T(8,128)S(1)} %fusion.2), channel_id=1, source_target_pairs={{0,8},{8,0},{1,9},{9,1},{2,10},{10,2},{3,11},{11,3},{4,12},{12,4},... | collective-permute-start | bytes 786440 | tf_op jit(solution)/shard_map/ppermute | solution.py:142
  128.2 1.1 collective-permute-done.1
  129.4 0.4 convolution_add_fusion
  129.8 15.8 %all_to_all.33 = f32[8,32,256]{2,1,0:T(8,128)S(1)} all-to-all(f32[8,32,256]{2,1,0:T(8,128)S(1)} %bitcast.31), channel_id=1, replica_groups=mesh['yh'=4,'y0'=2,'h'=2,'l'=2,'c'=2,'x'=4,'zl'=2] {'yh','y0'}, dimensions={0} | all-to-all | bytes 524288 | tf_op jit(solution)/shard_map/all_to_all | solution.py:143
  145.6 0.6 reduce_sum.29
  (10 shorter events, 0.2 us)
Async XLA Ops:
  1.3 14.2 %all-to-all-start = ((f32[4,3,128]{2,1,0:T(4,128)}), f32[4,3,128]{2,1,0:T(4,128)S(1)}, u32[]{:S(2)}, u32[]{:S(2)}) async-start(f32[4,3,128]{2,1,0:T(4,128)} %broadcast_in_dim.17), calls=%async_computation | async-start | bytes 16384 | tf_op jit(solution)/shard_map/all_to_all | solution.py:107
  10.0 5.5 %copy-start.1 = (f32[3,128]{1,0:T(4,128)S(1)}, f32[3,128]{1,0:T(4,128)}, u32[]{:S(2)}) copy-start(f32[3,128]{1,0:T(4,128)} %param.4) | copy-start | bytes 4612
  15.7 32.6 %copy-start = (f32[256,128]{1,0:T(8,128)S(1)}, f32[256,128]{1,0:T(8,128)}, u32[]{:S(2)}) copy-start(f32[256,128]{1,0:T(8,128)} %param.6) | copy-start | bytes 393220
  49.1 23.8 %collective-permute-start = (f32[8,208,128]{2,1,0:T(8,128)S(1)}, f32[8,208,128]{2,1,0:T(8,128)S(1)}, u32[]{:S(2)}, u32[]{:S(2)}) collective-permute-start(f32[8,208,128]{2,1,0:T(8,128)S(1)} %all_to_all.30.own_ref), channel_id=1, source_target_pairs={{0,8},{8,0},{1,9},{9,1},{2,10},{10,2},{3,11},{11,3},{4,12},{12,4},... | collective-permute-start | bytes 2555912 | tf_op jit(solution)/shard_map/ppermute | solution.py:118
  53.9 18.7 %all-to-all-start.2 = ((f32[4,256,128]{2,1,0:T(8,128)}), f32[4,256,128]{2,1,0:T(8,128)S(1)}, u32[]{:S(2)}, u32[]{:S(2)}) async-start(f32[4,256,128]{2,1,0:T(8,128)} %broadcast_in_dim.16), calls=%async_computation.2 | async-start | bytes 1048576 | tf_op jit(solution)/shard_map/all_to_all | solution.py:126
  122.3 7.1 %collective-permute-start.1 = (f32[256,256]{1,0:T(8,128)S(1)}, f32[256,256]{1,0:T(8,128)S(1)}, u32[]{:S(2)}, u32[]{:S(2)}) collective-permute-start(f32[256,256]{1,0:T(8,128)S(1)} %fusion.2), channel_id=1, source_target_pairs={{0,8},{8,0},{1,9},{9,1},{2,10},{10,2},{3,11},{11,3},{4,12},{12,4},... | collective-permute-start | bytes 786440 | tf_op jit(solution)/shard_map/ppermute | solution.py:142

commit v8 on v7

--- a/solution.py
+++ b/solution.py
@@ -13,7 +13,7 @@
 VEC = ("x", "zl")
 SWAP = [(0, 1), (1, 0)]
 BF16 = jnp.bfloat16
-TAIL = 16
+TAIL = 8
 
 
 def copies(block, peers):
@@ -29,7 +29,8 @@
     return lax.dot_general(a, b, (((1,), (1,)), ((), ())), preferred_element_type=jnp.float32)
 
 
-def pair_matmul_kernel(origin_ref, own_ref, other_ref, src_ref, out_ref, hi_ref, lo_ref):
+def pair_matmul_kernel(first_ref, origin_ref, own_ref, other_ref, src_ref, *rest):
+    out_ref, hi_ref, lo_ref = rest[-3:]
     blocks, _, half = own_ref.shape
     rows = out_ref.shape[1]
     origin = [origin_ref[comp : comp + 1, 0:1] for comp in range(3)]
@@ -72,27 +73,44 @@
     out_ref[0] = (0.5 * z).T
 
 
-def pair_matmul(origin, own, other, src):
+def pair_matmul(first, origin, own, other, src, peers, *earlier):
     blocks, height, half = own.shape
     rows = (height - TAIL) // 3
-    peers, _, per = src.shape
-    pairs = peers * per * 2 * half * blocks
+    given, _, per = src.shape
+    lead = len(earlier)
+    steps = peers - 1 if lead else 1
+    pairs = steps * per * 2 * half * blocks
+
+    def where(i, f):
+        return ((i + lead + f[0]) % peers, 0, 0)
+
+    vmem = pl.BlockSpec(memory_space=pltpu.VMEM)
     return pl.pallas_call(
         pair_matmul_kernel,
         out_shape=jax.ShapeDtypeStruct((peers, rows, per), jnp.float32),
-        grid=(peers,),
-        in_specs=[pl.BlockSpec(memory_space=pltpu.VMEM)] * 3 + [pl.BlockSpec((1, 8, per), lambda i: (i, 0, 0))],
-        out_specs=pl.BlockSpec((1, rows, per), lambda i: (i, 0, 0)),
-        scratch_shapes=[pltpu.VMEM((blocks, 4 * rows, 2 * half), BF16)] * 2,
+        grid_spec=pltpu.PrefetchScalarGridSpec(
+            num_scalar_prefetch=1,
+            grid=(steps,),
+            in_specs=[vmem] * 3
+            + [pl.BlockSpec((1, 8, per), where if given > 1 else lambda i, f: (0, 0, 0))]
+            + [pl.BlockSpec(memory_space=pl.ANY)] * lead,
+            out_specs=pl.BlockSpec((1, rows, per), where),
+            scratch_shapes=[pltpu.VMEM((blocks, 4 * rows, 2 * half), BF16)] * 2,
+        ),
+        input_output_aliases={5: 0} if lead else {},
         compiler_params=pltpu.CompilerParams(
             dimension_semantics=("arbitrary",), vmem_limit_bytes=32 * 1024 * 1024
         ),
         cost_estimate=pl.CostEstimate(
             flops=pairs * 4 * rows * 2 * 3,
-            bytes_accessed=2 * blocks * height * half * 4 + peers * rows * per * 4,
+            bytes_accessed=2 * blocks * height * half * 4 + steps * rows * per * 4,
             transcendentals=2 * pairs,
         ),
-    )(origin, own, other, src)
+    )(first, origin, own, other, src, *earlier)
+
+
+def origin_of(src):
+    return jnp.broadcast_to(jnp.mean(src, axis=(0, 2))[:, None], (8, 128))
 
 
 def body(tgt_coords, src_coords, src_values, grad_vectors):
@@ -104,28 +122,27 @@
     piece = rows // n["c"]
     c = lax.axis_index("c")
 
-    src_y = lax.all_to_all(copies(src_coords, n["yh"]), "yh", 0, 0, tiled=True)
-    src_y = src_y.reshape(3 * n["yh"], pts)
     rowmajor = Layout(major_to_minor=(0, 1, 2))
     values = with_layout_constraint(copies(src_values, nz), rowmajor)
 
     grads = grad_vectors.reshape(3, nz, rows, pts).transpose(1, 0, 2, 3).reshape(nz, 3 * rows, pts)
-    tail = jnp.concatenate([tgt_coords, src_y, jnp.zeros((1, pts), jnp.float32)], axis=0)
+    tail = jnp.concatenate([tgt_coords, src_coords, jnp.zeros((TAIL - 6, pts), jnp.float32)], axis=0)
     load = jnp.concatenate([grads, copies(tail, nz)], axis=1)
     load = copies(load, n["y0"]).reshape(n["y0"] * nz, 3 * rows + TAIL, pts)
     own = lax.all_to_all(load, ("y0", "h", "l"), 0, 0, tiled=True)
-    values, own = lax.optimization_barrier((values, own))
     other = lax.ppermute(own, "c", SWAP)
 
-    near = own[:, 3 * rows + 3 : 3 * rows + 3 + 3 * n["yh"], :].reshape(n["y0"], nz, n["yh"], 3, pts)
+    near = own[:, 3 * rows + 3 : 3 * rows + 6, :].reshape(n["y0"], nz, 3, pts)
     near = lax.dynamic_index_in_dim(near, lax.axis_index("y0"), 0, False)
-    src = near.transpose(1, 2, 0, 3).reshape(n["yh"], 3, nz * pts)
-    src = jnp.pad(src, ((0, 0), (0, 5), (0, 0)))
-    origin = jnp.broadcast_to(jnp.mean(src, axis=(0, 2))[:, None], (8, pts))
+    near = jnp.pad(near.transpose(1, 0, 2).reshape(3, nz * pts), ((0, 5), (0, 0)))
+    first = lax.axis_index("yh").astype(jnp.int32).reshape(1)
+    src = lax.all_to_all(copies(near, n["yh"]), "yh", 0, 0, tiled=True)
+    partial_z = pair_matmul(first, origin_of(near[None]), own, other, near[None], n["yh"])
+    src, values, partial_z = lax.optimization_barrier((src, values, partial_z))
 
     values = with_layout_constraint(lax.all_to_all(values, ("h", "l"), 0, 0, tiled=True), rowmajor)
 
-    partial_z = pair_matmul(origin, own, other, src)
+    partial_z = pair_matmul(first, origin_of(src), own, other, src, n["yh"], partial_z)
     spts = partial_z.shape[2]
     values = values.transpose(1, 0, 2).reshape(slab, spts)
     partial_z, values, south = lax.optimization_barrier((partial_z, values, c == 0))

time: 147 us -> 132 us (0.90)
  the two profiles are of different devices: /device:TPU:1 before, /device:TPU:128 now
where the time goes in v8:
time: 132 us
  blocking collectives  86.7 us (66%)
  Pallas kernels  15.8 us (12%)
  starting transfers between devices  15.4 us (12%)
  waiting for transfers between devices  8.3 us (6%)
  local copies, waits for them, and re-layouts  3.78 us (3%)
    all_to_all x1, blocking collectives, body(): own = lax.all_to_all(load, ('y0', 'h', 'l'), 0, 0, tiled=True)  31.6 us
    all_to_all x1, blocking collectives, body(): arrived = lax.all_to_all(partial_z, 'yh', 0, 0, tiled=True)  20.9 us
    all_to_all x1, blocking collectives, body(): lax.all_to_all(part.reshape(nv, piece, slab), ('yh', 'y0'), 0, 0, tiled=T...  18.5 us
    pallas_call x2, Pallas kernels, pair_matmul(): pl.pallas_call(pair_matmul_kernel, out_shape=jax.ShapeDtypeStruct((peers,...  15.8 us
    all_to_all x1, blocking collectives, body(): lax.all_to_all(copies(z, nv), VEC, 0, 0, tiled=True)  15.6 us
    all_to_all x1, starting transfers between devices, body(): src = lax.all_to_all(copies(near, n['yh']), 'yh', 0, 0, tiled=True)  6.19 us
    all_to_all x1, starting transfers between devices, body(): lax.all_to_all(values, ('h', 'l'), 0, 0, tiled=True)  5.4 us
    all_to_all x1, waiting for transfers between devices, body(): src = lax.all_to_all(copies(near, n['yh']), 'yh', 0, 0, tiled=True)  4.29 us
  transfers between devices with their start and end apart: 4, of which 3 were waited for; matrix products, arithmetic and copies ran while one was open for 1% of the time, Pallas kernels for 12%

profile of v8, /device:TPU:128, one launch (start us, length us, event | category | flops | bytes accessed | tf_op | source)
XLA Modules:
  0.0 131.9 jit_solution(10517162387705234385)
XLA Ops:
  0.0 0.0 copy-start.2
  0.0 1.0 copy.8
  1.0 0.0 copy-start.1
  1.1 0.1 pad.9.clone
  1.1 0.0 copy-done.2
  1.1 0.6 copy-done.1
  1.7 0.1 maximum_maximum_fusion
  1.8 0.1 broadcast_in_dim.22
  1.9 31.6 %all_to_all.30.own_ref = f32[8,200,128]{2,1,0:T(8,128)S(1)} all-to-all(f32[8,200,128]{2,1,0:T(8,128)S(1)} %bitcast.33), channel_id=1, replica_groups=mesh['yh'=4,'y0'=2,'h'=2,'l'=2,'c'=2,'x'=4,'zl'=2] {'y0','h','l'}, dimensions={0} | all-to-all | bytes 1638400 | tf_op jit(solution)/shard_map/all_to_all | solution.py:132
  33.5 1.9 %collective-permute-start = (f32[8,200,128]{2,1,0:T(8,128)S(1)}, f32[8,200,128]{2,1,0:T(8,128)S(1)}, u32[]{:S(2)}, u32[]{:S(2)}) collective-permute-start(f32[8,200,128]{2,1,0:T(8,128)S(1)} %all_to_all.30.own_ref), channel_id=1, source_target_pairs={{0,8},{8,0},{1,9},{9,1},{2,10},{10,2},{3,11},{11,3},{4,12},{12,4},... | collective-permute-start | bytes 2457608 | tf_op jit(solution)/shard_map/ppermute | solution.py:133
  35.5 0.1 pad_bitcast_fusion
  35.6 0.6 broadcast_in_dim.23
  36.2 6.2 %all-to-all-start.1 = ((f32[4,8,512]{2,1,0:T(8,128)}), f32[4,8,512]{2,1,0:T(8,128)S(1)}, u32[]{:S(2)}, u32[]{:S(2)}) async-start(f32[4,8,512]{2,1,0:T(8,128)} %broadcast_in_dim.23), calls=%async_computation.1 | async-start | bytes 131072 | tf_op jit(solution)/shard_map/all_to_all | solution.py:139
  42.4 0.0 collective-permute-done.other_ref
  42.4 0.1 broadcast_in_dim.25.origin_ref
  42.5 0.0 copy-start
  42.5 4.2 %shard_map.46.rest_0_ = f32[4,64,512]{2,1,0:T(8,128)S(1)} custom-call(s32[1]{0:T(128)} %bitcast.first_ref, f32[8,128]{1,0:T(8,128)S(1)} %broadcast_in_dim.25.origin_ref, f32[8,200,128]{2,1,0:T(8,128)S(1)} %all_to_all.30.own_ref, f32[8,200,128]{2,1,0:T(8,128)S(1)} %collective-permute-done.other_ref, f32[1,8,512]{2,1,0:T(8,128)S(1)} %get-tuple-element.19.src_ref), custom_call_target="tpu_custom_call" | custom-call | flops 1610612736 | bytes 1769472 | tf_op jit(solution)/shard_map/pallas_call | solution.py:88
  46.7 4.3 %all-to-all-done.1.src_ref = f32[4,8,512]{2,1,0:T(8,128)S(1)} async-done(((f32[4,8,512]{2,1,0:T(8,128)}), f32[4,8,512]{2,1,0:T(8,128)S(1)}, u32[]{:S(2)}, u32[]{:S(2)}) %all-to-all-start.1) | async-done | bytes 65568 | tf_op jit(solution)/shard_map/all_to_all | solution.py:139
  51.0 0.0 copy-done
  51.0 0.8 broadcast_in_dim.24
  51.8 5.4 %all-to-all-start.2 = ((f32[4,256,128]{2,1,0:T(8,128)}), f32[4,256,128]{2,1,0:T(8,128)S(1)}, u32[]{:S(2)}, u32[]{:S(2)}) async-start(f32[4,256,128]{2,1,0:T(8,128)} %broadcast_in_dim.24), calls=%async_computation.2 | async-start | bytes 1048576 | tf_op jit(solution)/shard_map/all_to_all | solution.py:143
  57.2 0.1 reduce_sum.37
  57.4 0.1 broadcast_in_dim.27.origin_ref
  57.4 11.6 %shard_map.47 = f32[4,64,512]{2,1,0:T(8,128)S(1)} custom-call(s32[1]{0:T(128)} %bitcast.first_ref, f32[8,128]{1,0:T(8,128)S(1)} %broadcast_in_dim.27.origin_ref, f32[8,200,128]{2,1,0:T(8,128)S(1)} %all_to_all.30.own_ref, f32[8,200,128]{2,1,0:T(8,128)S(1)} %collective-permute-done.other_ref, ...), custom_call_target="tpu_custom_call", output_to_operand_aliasing={{}: (5, {})} | custom-call | flops 4831838208 | bytes 2031616 | tf_op jit(solution)/shard_map/pallas_call | solution.py:88
  69.0 2.5 %all-to-all-done.2 = f32[4,256,128]{2,1,0:T(8,128)S(1)} async-done(((f32[4,256,128]{2,1,0:T(8,128)}), f32[4,256,128]{2,1,0:T(8,128)S(1)}, u32[]{:S(2)}, u32[]{:S(2)}) %all-to-all-start.2) | async-done | bytes 524320 | tf_op jit(solution)/shard_map/all_to_all | solution.py:143
  71.5 0.2 copy.10
  71.7 20.9 %all_to_all.31 = f32[4,64,512]{2,1,0:T(8,128)S(1)} all-to-all(f32[4,64,512]{2,1,0:T(8,128)S(1)} %shard_map.47), channel_id=1, replica_groups=mesh['yh'=4,'y0'=2,'h'=2,'l'=2,'c'=2,'x'=4,'zl'=2] {'yh'}, dimensions={0} | all-to-all | bytes 1048576 | tf_op jit(solution)/shard_map/all_to_all | solution.py:150
  92.7 0.1 broadcast_in_dim.29
  92.8 15.6 %all_to_all.32 = f32[8,64,512]{2,1,0:T(8,128)S(1)} all-to-all(f32[8,64,512]{2,1,0:T(8,128)S(1)} %broadcast_in_dim.29), channel_id=1, replica_groups=mesh['yh'=4,'y0'=2,'h'=2,'l'=2,'c'=2,'x'=4,'zl'=2] {'x','zl'}, dimensions={0} | all-to-all | bytes 2097152 | tf_op jit(solution)/shard_map/all_to_all | solution.py:153
  108.4 0.1 fusion
  108.5 0.4 fusion.1
  108.9 1.9 %collective-permute-start.1 = (f32[256,256]{1,0:T(8,128)S(1)}, f32[256,256]{1,0:T(8,128)S(1)}, u32[]{:S(2)}, u32[]{:S(2)}) collective-permute-start(f32[256,256]{1,0:T(8,128)S(1)} %fusion.1), channel_id=1, source_target_pairs={{0,8},{8,0},{1,9},{9,1},{2,10},{10,2},{3,11},{11,3},{4,12},{12,4},... | collective-permute-start | bytes 786440 | tf_op jit(solution)/shard_map/ppermute | solution.py:159
  110.8 1.5 %collective-permute-done.1 = f32[256,256]{1,0:T(8,128)S(1)} collective-permute-done((f32[256,256]{1,0:T(8,128)S(1)}, f32[256,256]{1,0:T(8,128)S(1)}, u32[]{:S(2)}, u32[]{:S(2)}) %collective-permute-start.1) | collective-permute-done | bytes 262176 | tf_op jit(solution)/shard_map/ppermute | solution.py:159
  112.3 0.4 convolution_add_fusion
  112.7 18.5 %all_to_all.33 = f32[8,32,256]{2,1,0:T(8,128)S(1)} all-to-all(f32[8,32,256]{2,1,0:T(8,128)S(1)} %bitcast.38), channel_id=1, replica_groups=mesh['yh'=4,'y0'=2,'h'=2,'l'=2,'c'=2,'x'=4,'zl'=2] {'yh','y0'}, dimensions={0} | all-to-all | bytes 524288 | tf_op jit(solution)/shard_map/all_to_all | solution.py:160
  131.3 0.6 reduce_sum.39
  (11 shorter events, 0.1 us)
Async XLA Ops:
  0.0 1.1 copy-start.2
  1.0 0.7 copy-start.1
  33.5 8.9 %collective-permute-start = (f32[8,200,128]{2,1,0:T(8,128)S(1)}, f32[8,200,128]{2,1,0:T(8,128)S(1)}, u32[]{:S(2)}, u32[]{:S(2)}) collective-permute-start(f32[8,200,128]{2,1,0:T(8,128)S(1)} %all_to_all.30.own_ref), channel_id=1, source_target_pairs={{0,8},{8,0},{1,9},{9,1},{2,10},{10,2},{3,11},{11,3},{4,12},{12,4},... | collective-permute-start | bytes 2457608 | tf_op jit(solution)/shard_map/ppermute | solution.py:133
  36.2 14.8 %all-to-all-start.1 = ((f32[4,8,512]{2,1,0:T(8,128)}), f32[4,8,512]{2,1,0:T(8,128)S(1)}, u32[]{:S(2)}, u32[]{:S(2)}) async-start(f32[4,8,512]{2,1,0:T(8,128)} %broadcast_in_dim.23), calls=%async_computation.1 | async-start | bytes 131072 | tf_op jit(solution)/shard_map/all_to_all | solution.py:139
  42.5 8.5 %copy-start = (f32[256,128]{1,0:T(8,128)S(1)}, f32[256,128]{1,0:T(8,128)}, u32[]{:S(2)}) copy-start(f32[256,128]{1,0:T(8,128)} %param.6) | copy-start | bytes 393220
  51.8 19.7 %all-to-all-start.2 = ((f32[4,256,128]{2,1,0:T(8,128)}), f32[4,256,128]{2,1,0:T(8,128)S(1)}, u32[]{:S(2)}, u32[]{:S(2)}) async-start(f32[4,256,128]{2,1,0:T(8,128)} %broadcast_in_dim.24), calls=%async_computation.2 | async-start | bytes 1048576 | tf_op jit(solution)/shard_map/all_to_all | solution.py:143
  108.9 3.4 %collective-permute-start.1 = (f32[256,256]{1,0:T(8,128)S(1)}, f32[256,256]{1,0:T(8,128)S(1)}, u32[]{:S(2)}, u32[]{:S(2)}) collective-permute-start(f32[256,256]{1,0:T(8,128)S(1)} %fusion.1), channel_id=1, source_target_pairs={{0,8},{8,0},{1,9},{9,1},{2,10},{10,2},{3,11},{11,3},{4,12},{12,4},... | collective-permute-start | bytes 786440 | tf_op jit(solution)/shard_map/ppermute | solution.py:159

commit v9 on v7

--- a/solution.py
+++ b/solution.py
@@ -112,13 +112,12 @@
     grads = grad_vectors.reshape(3, nz, rows, pts).transpose(1, 0, 2, 3).reshape(nz, 3 * rows, pts)
     tail = jnp.concatenate([tgt_coords, src_y, jnp.zeros((1, pts), jnp.float32)], axis=0)
     load = jnp.concatenate([grads, copies(tail, nz)], axis=1)
-    load = copies(load, n["y0"]).reshape(n["y0"] * nz, 3 * rows + TAIL, pts)
-    own = lax.all_to_all(load, ("y0", "h", "l"), 0, 0, tiled=True)
-    values, own = lax.optimization_barrier((values, own))
+    own = lax.all_to_all(load, ("h", "l"), 0, 0, tiled=True)
+    far = lax.ppermute(own, "y0", SWAP)
+    near = own[:, 3 * rows + 3 : 3 * rows + 3 + 3 * n["yh"], :].reshape(nz, n["yh"], 3, pts)
+    values, near = lax.optimization_barrier((values, near))
+    own = jnp.concatenate([own, far], axis=0)
     other = lax.ppermute(own, "c", SWAP)
-
-    near = own[:, 3 * rows + 3 : 3 * rows + 3 + 3 * n["yh"], :].reshape(n["y0"], nz, n["yh"], 3, pts)
-    near = lax.dynamic_index_in_dim(near, lax.axis_index("y0"), 0, False)
     src = near.transpose(1, 2, 0, 3).reshape(n["yh"], 3, nz * pts)
     src = jnp.pad(src, ((0, 0), (0, 5), (0, 0)))
     origin = jnp.broadcast_to(jnp.mean(src, axis=(0, 2))[:, None], (8, pts))

time: 147 us -> 150 us (1.020)
  blocking collectives: 81.8 us -> 75.4 us
  starting transfers between devices: 21.8 us -> 28 us
  waiting for transfers between devices: 21.6 us -> 25.2 us
    all_to_all x1, blocking collectives: 32.6 us -> 19.9 us  [body(): own = lax.all_to_all(load, ('h', 'l'), 0, 0, tiled=True)]
    all_to_all x1, blocking collectives: 16.5 us -> 24.1 us  [body(): lax.all_to_all(copies(z, nv), VEC, 0, 0, tiled=True)]
    ppermute x0 -> x1, waiting for transfers between devices: none -> 6.52 us  [body(): far = lax.ppermute(own, 'y0', SWAP)]
    ppermute x1, starting transfers between devices: 4.79 us -> 9.38 us  [body(): other = lax.ppermute(own, 'c', SWAP)]
    all_to_all x1, waiting for transfers between devices: 15 us -> 12 us  [body(): lax.all_to_all(values, ('h', 'l'), 0, 0, tiled=True)]
    ppermute x0 -> x1, starting transfers between devices: none -> 2.29 us  [body(): far = lax.ppermute(own, 'y0', SWAP)]
  transfers between devices with their start and end apart: 4 -> 5, of which waited for: 3 -> 4; matrix products, arithmetic and copies ran while one was open for 1% -> 2% of each run, Pallas kernels for 0% -> 0%
where the time goes in v9:
time: 150 us; the launch traced here: 149 us
  blocking collectives  75.4 us (50%)
  starting transfers between devices  28 us (19%)
  waiting for transfers between devices  25.2 us (17%)
  Pallas kernels  15.3 us (10%)
  local copies, waits for them, and re-layouts  3.79 us (3%)
    all_to_all x1, blocking collectives, body(): lax.all_to_all(copies(z, nv), VEC, 0, 0, tiled=True)  24.1 us
    all_to_all x1, blocking collectives, body(): own = lax.all_to_all(load, ('h', 'l'), 0, 0, tiled=True)  19.9 us
    all_to_all x1, blocking collectives, body(): arrived = lax.all_to_all(partial_z, 'yh', 0, 0, tiled=True)  16.6 us
    pallas_call x1, Pallas kernels, pair_matmul(): pl.pallas_call(pair_matmul_kernel, out_shape=jax.ShapeDtypeStruct((peers,...  15.3 us
    all_to_all x1, blocking collectives, body(): lax.all_to_all(part.reshape(nv, piece, slab), ('yh', 'y0'), 0, 0, tiled=T...  14.8 us
    all_to_all x1, waiting for transfers between devices, body(): lax.all_to_all(values, ('h', 'l'), 0, 0, tiled=True)  12 us
    ppermute x1, starting transfers between devices, body(): other = lax.ppermute(own, 'c', SWAP)  9.38 us
    all_to_all x1, starting transfers between devices, body(): src_y = lax.all_to_all(copies(src_coords, n['yh']), 'yh', 0, 0, tiled=True)  7.63 us
  transfers between devices with their start and end apart: 5, of which 4 were waited for; matrix products, arithmetic and copies ran while one was open for 2% of the time, Pallas kernels for 0%

profile of v9, /device:TPU:1, one launch (start us, length us, event | category | flops | bytes accessed | tf_op | source)
XLA Modules:
  0.0 149.4 jit_solution(6620329994728770918)
XLA Ops:
  0.0 1.3 broadcast_in_dim.15
  1.3 7.6 %all-to-all-start = ((f32[4,3,128]{2,1,0:T(4,128)}), f32[4,3,128]{2,1,0:T(4,128)S(1)}, u32[]{:S(2)}, u32[]{:S(2)}) async-start(f32[4,3,128]{2,1,0:T(4,128)} %broadcast_in_dim.15), calls=%async_computation | async-start | bytes 16384 | tf_op jit(solution)/shard_map/all_to_all | solution.py:107
  8.9 1.0 copy.7
  9.9 0.1 pad.9.clone
  10.0 0.0 copy-start.1
  10.0 5.5 %all-to-all-done = f32[4,3,128]{2,1,0:T(4,128)S(1)} async-done(((f32[4,3,128]{2,1,0:T(4,128)}), f32[4,3,128]{2,1,0:T(4,128)S(1)}, u32[]{:S(2)}, u32[]{:S(2)}) %all-to-all-start) | async-done | bytes 6176 | tf_op jit(solution)/shard_map/all_to_all | solution.py:107
  15.5 0.0 copy-done.1
  15.5 0.1 maximum_maximum_fusion
  15.6 19.9 %all_to_all.30 = f32[4,208,128]{2,1,0:T(8,128)S(1)} all-to-all(f32[4,208,128]{2,1,0:T(8,128)S(1)} %pad_maximum_fusion), channel_id=1, replica_groups=mesh['yh'=4,'y0'=2,'h'=2,'l'=2,'c'=2,'x'=4,'zl'=2] {'h','l'}, dimensions={0} | all-to-all | bytes 851968 | tf_op jit(solution)/shard_map/all_to_all | solution.py:115
  35.5 2.3 %collective-permute-start = (f32[4,208,128]{2,1,0:T(8,128)S(1)}, f32[4,208,128]{2,1,0:T(8,128)S(1)}, u32[]{:S(2)}, u32[]{:S(2)}) collective-permute-start(f32[4,208,128]{2,1,0:T(8,128)S(1)} %all_to_all.30), channel_id=1, source_target_pairs={{0,64},{64,0},{1,65},{65,1},{2,66},{66,2},{3,67},{67,3},{4,68},{68... | collective-permute-start | bytes 1277960 | tf_op jit(solution)/shard_map/ppermute | solution.py:116
  37.8 6.5 %collective-permute-done = f32[4,208,128]{2,1,0:T(8,128)S(1)} collective-permute-done((f32[4,208,128]{2,1,0:T(8,128)S(1)}, f32[4,208,128]{2,1,0:T(8,128)S(1)}, u32[]{:S(2)}, u32[]{:S(2)}) %collective-permute-start) | collective-permute-done | bytes 426016 | tf_op jit(solution)/shard_map/ppermute | solution.py:116
  44.3 0.0 copy-start
  44.4 9.4 %collective-permute-start.1 = (f32[8,208,128]{2,1,0:T(8,128)S(1)}, f32[8,208,128]{2,1,0:T(8,128)S(1)}, u32[]{:S(2)}, u32[]{:S(2)}) collective-permute-start(f32[8,208,128]{2,1,0:T(8,128)S(1)} %constant_dynamic-update-slice_fusion.own_ref), channel_id=1, source_target_pairs={{0,8},{8,0},{1,9},{9,1},{2,10},{10,2},{3,11},{11,3},{4,12},{12,4},... | collective-permute-start | bytes 2555912 | tf_op jit(solution)/shard_map/ppermute | solution.py:120
  53.8 0.0 copy-done
  53.8 0.8 broadcast_in_dim.14
  54.6 3.5 %all-to-all-start.2 = ((f32[4,256,128]{2,1,0:T(8,128)}), f32[4,256,128]{2,1,0:T(8,128)S(1)}, u32[]{:S(2)}, u32[]{:S(2)}) async-start(f32[4,256,128]{2,1,0:T(8,128)} %broadcast_in_dim.14), calls=%async_computation.2 | async-start | bytes 1048576 | tf_op jit(solution)/shard_map/all_to_all | solution.py:125
  58.2 0.1 fusion.1
  58.3 12.0 %all-to-all-done.2 = f32[4,256,128]{2,1,0:T(8,128)S(1)} async-done(((f32[4,256,128]{2,1,0:T(8,128)}), f32[4,256,128]{2,1,0:T(8,128)S(1)}, u32[]{:S(2)}, u32[]{:S(2)}) %all-to-all-start.2) | async-done | bytes 524320 | tf_op jit(solution)/shard_map/all_to_all | solution.py:125
  70.3 0.2 copy.11
  70.5 0.0 collective-permute-done.1.other_ref
  70.5 0.1 broadcast_in_dim.18.origin_ref
  70.6 15.3 %shard_map.46 = f32[4,64,512]{2,1,0:T(8,128)S(1)} custom-call(f32[8,128]{1,0:T(8,128)S(1)} %broadcast_in_dim.18.origin_ref, f32[8,208,128]{2,1,0:T(8,128)S(1)} %constant_dynamic-update-slice_fusion.own_ref, f32[8,208,128]{2,1,0:T(8,128)S(1)} %collective-permute-done.1.other_ref, f32[4,8,512]{2,1,0:T(8,128)S(1)} %get-tuple-element.17.src_ref), custom_call_target="tpu_custom_call" | custom-call | flops 6442450944 | bytes 2228224 | tf_op jit(solution)/shard_map/pallas_call | solution.py:80
  85.9 16.6 %all_to_all.31 = f32[4,64,512]{2,1,0:T(8,128)S(1)} all-to-all(f32[4,64,512]{2,1,0:T(8,128)S(1)} %shard_map.46), channel_id=1, replica_groups=mesh['yh'=4,'y0'=2,'h'=2,'l'=2,'c'=2,'x'=4,'zl'=2] {'yh'}, dimensions={0} | all-to-all | bytes 1048576 | tf_op jit(solution)/shard_map/all_to_all | solution.py:132
  102.5 0.1 broadcast_in_dim.40
  102.6 24.1 %all_to_all.32 = f32[8,64,512]{2,1,0:T(8,128)S(1)} all-to-all(f32[8,64,512]{2,1,0:T(8,128)S(1)} %broadcast_in_dim.40), channel_id=1, replica_groups=mesh['yh'=4,'y0'=2,'h'=2,'l'=2,'c'=2,'x'=4,'zl'=2] {'x','zl'}, dimensions={0} | all-to-all | bytes 2097152 | tf_op jit(solution)/shard_map/all_to_all | solution.py:135
  126.8 0.1 fusion
  126.8 0.4 fusion.2
  127.2 5.2 %collective-permute-start.2 = (f32[256,256]{1,0:T(8,128)S(1)}, f32[256,256]{1,0:T(8,128)S(1)}, u32[]{:S(2)}, u32[]{:S(2)}) collective-permute-start(f32[256,256]{1,0:T(8,128)S(1)} %fusion.2), channel_id=1, source_target_pairs={{0,8},{8,0},{1,9},{9,1},{2,10},{10,2},{3,11},{11,3},{4,12},{12,4},... | collective-permute-start | bytes 786440 | tf_op jit(solution)/shard_map/ppermute | solution.py:141
  132.5 1.1 collective-permute-done.2
  133.6 0.4 convolution_add_fusion
  134.0 14.8 %all_to_all.33 = f32[8,32,256]{2,1,0:T(8,128)S(1)} all-to-all(f32[8,32,256]{2,1,0:T(8,128)S(1)} %bitcast.26), channel_id=1, replica_groups=mesh['yh'=4,'y0'=2,'h'=2,'l'=2,'c'=2,'x'=4,'zl'=2] {'yh','y0'}, dimensions={0} | all-to-all | bytes 524288 | tf_op jit(solution)/shard_map/all_to_all | solution.py:142
  148.8 0.6 reduce_sum.29
  (11 shorter events, 0.2 us)
Async XLA Ops:
  1.3 14.2 %all-to-all-start = ((f32[4,3,128]{2,1,0:T(4,128)}), f32[4,3,128]{2,1,0:T(4,128)S(1)}, u32[]{:S(2)}, u32[]{:S(2)}) async-start(f32[4,3,128]{2,1,0:T(4,128)} %broadcast_in_dim.15), calls=%async_computation | async-start | bytes 16384 | tf_op jit(solution)/shard_map/all_to_all | solution.py:107
  10.0 5.5 %copy-start.1 = (f32[3,128]{1,0:T(4,128)S(1)}, f32[3,128]{1,0:T(4,128)}, u32[]{:S(2)}) copy-start(f32[3,128]{1,0:T(4,128)} %param.4) | copy-start | bytes 4612
  35.5 8.9 %collective-permute-start = (f32[4,208,128]{2,1,0:T(8,128)S(1)}, f32[4,208,128]{2,1,0:T(8,128)S(1)}, u32[]{:S(2)}, u32[]{:S(2)}) collective-permute-start(f32[4,208,128]{2,1,0:T(8,128)S(1)} %all_to_all.30), channel_id=1, source_target_pairs={{0,64},{64,0},{1,65},{65,1},{2,66},{66,2},{3,67},{67,3},{4,68},{68... | collective-permute-start | bytes 1277960 | tf_op jit(solution)/shard_map/ppermute | solution.py:116
  44.3 9.5 %copy-start = (f32[256,128]{1,0:T(8,128)S(1)}, f32[256,128]{1,0:T(8,128)}, u32[]{:S(2)}) copy-start(f32[256,128]{1,0:T(8,128)} %param.6) | copy-start | bytes 393220
  44.4 26.1 %collective-permute-start.1 = (f32[8,208,128]{2,1,0:T(8,128)S(1)}, f32[8,208,128]{2,1,0:T(8,128)S(1)}, u32[]{:S(2)}, u32[]{:S(2)}) collective-permute-start(f32[8,208,128]{2,1,0:T(8,128)S(1)} %constant_dynamic-update-slice_fusion.own_ref), channel_id=1, source_target_pairs={{0,8},{8,0},{1,9},{9,1},{2,10},{10,2},{3,11},{11,3},{4,12},{12,4},... | collective-permute-start | bytes 2555912 | tf_op jit(solution)/shard_map/ppermute | solution.py:120
  54.6 15.7 %all-to-all-start.2 = ((f32[4,256,128]{2,1,0:T(8,128)}), f32[4,256,128]{2,1,0:T(8,128)S(1)}, u32[]{:S(2)}, u32[]{:S(2)}) async-start(f32[4,256,128]{2,1,0:T(8,128)} %broadcast_in_dim.14), calls=%async_computation.2 | async-start | bytes 1048576 | tf_op jit(solution)/shard_map/all_to_all | solution.py:125
  127.2 6.4 %collective-permute-start.2 = (f32[256,256]{1,0:T(8,128)S(1)}, f32[256,256]{1,0:T(8,128)S(1)}, u32[]{:S(2)}, u32[]{:S(2)}) collective-permute-start(f32[256,256]{1,0:T(8,128)S(1)} %fusion.2), channel_id=1, source_target_pairs={{0,8},{8,0},{1,9},{9,1},{2,10},{10,2},{3,11},{11,3},{4,12},{12,4},... | collective-permute-start | bytes 786440 | tf_op jit(solution)/shard_map/ppermute | solution.py:141
